TPU v7x, 128 devices: a whole 4x4x4 slice. The times are simulated.
128 devices in a mesh: gx: 8 (over y, x_lo), gy: 16 (over x_hi, z, core).
Axes of the slice: x: 4 (x_hi: 2, x_lo: 2; x = x_hi * 2 + x_lo), y: 4, z: 4, core: 2. Of those that a mesh axis runs over, the one named last changes fastest.
Arguments:
- right_side: float32 [512, 512, 256], P('gx', 'gy'), may hold values from -45 to 45
- block_inverse: float32 [1, 256, 256], replicated, may hold values from -1 to 2
- basis_left: float32 [2, 1, 32, 256], replicated, may hold values from -0.25 to 0.25
- basis_right: float32 [2, 1, 32, 256], replicated, may hold values from -0.25 to 0.25
- ranks: int32 [2, 1, 512, 512], replicated, may hold values from 1 to 32
Outputs:
- solution_field: float32 [512, 512, 256], P('gx', 'gy')
- true_gap: float32 [512, 512, 256], P('gx', 'gy')
- preconditioned: float32 [512, 512, 256], P('gx', 'gy')
All inputs are finite; a program needn't handle non-finite values.
Results may differ from a plain program's by a relative error of at most 0.0003.
Values sent between devices are 32-bit elements; how exact they have to be, the bound alone decides.
A program may use at most 64 MiB of HBM per device.

v0:
```python
import functools

import jax
import jax.numpy as jnp
from jax import lax
from jax.experimental import pallas as pl
from jax.experimental.pallas import tpu as pltpu
from jax.sharding import PartitionSpec as P

F32 = jnp.float32
BF16 = jnp.bfloat16
MESH = pl.DeviceIdType.MESH

mass_shift = 0.05

S_BU0, S_U0V0, S_BU1, S_V0U1, S_U1V1 = range(5)


def halves(value):
    high = value.astype(BF16)
    return high, (value - high.astype(F32)).astype(BF16)


def dot(a, b):
    return lax.dot_general(a, b, (((1,), (0,)), ((), ())), preferred_element_type=F32)


def fold(value):
    rows, width = value.shape
    return jnp.sum(value.reshape(rows // 8, 8, width), axis=0)


def kernel(
    devs, b_any, binv_any, left_any, right_any, ranks_any,
    x_out, gap_out, z_out,
    b, binv, bases, tiles, prev, wide, wb, wc, wd, picks, mask, split, dsplit,
    u0, u1, u2, v0, v1, c0, c1, c2,
    send_c, recv_c, send_u, recv_u, part, got_y, got_x,
    load_sem, send_sem, recv_sem, rsend_sem, rrecv_sem,
):
    ndx, ndy = devs
    nx, ny, nz = b.shape
    gx = lax.axis_index("gx")
    gy = lax.axis_index("gy")
    east, west = lax.rem(gx + 1, ndx), lax.rem(gx + ndx - 1, ndx)
    north, south = lax.rem(gy + 1, ndy), lax.rem(gy + ndy - 1, ndy)

    barrier = pltpu.get_barrier_semaphore()
    for k in range(1, ndy):
        pl.semaphore_signal(barrier, 1, device_id=(gx, lax.rem(gy + k, ndy)), device_id_type=MESH)
    for k in range(1, ndx):
        pl.semaphore_signal(barrier, 1, device_id=(lax.rem(gx + k, ndx), gy), device_id_type=MESH)

    per_tile = 128 // ny
    col = pl.multiple_of(gy // per_tile * 128, 128)
    col_back = pl.multiple_of(south // per_tile * 128, 128)
    row = pl.multiple_of(gx * nx, 8)
    row_back = pl.multiple_of(west * nx + nx - 8, 8)
    loads = [
        pltpu.make_async_copy(binv_any.at[0], binv, load_sem.at[0]),
        pltpu.make_async_copy(right_any.at[0, 0], bases.at[0], load_sem.at[1]),
        pltpu.make_async_copy(left_any.at[0, 0], bases.at[1], load_sem.at[2]),
        pltpu.make_async_copy(right_any.at[1, 0], bases.at[2], load_sem.at[3]),
        pltpu.make_async_copy(left_any.at[1, 0], bases.at[3], load_sem.at[4]),
        pltpu.make_async_copy(ranks_any.at[0, 0, pl.ds(row, nx), pl.ds(col, 128)], tiles.at[0], load_sem.at[5]),
        pltpu.make_async_copy(ranks_any.at[1, 0, pl.ds(row, nx), pl.ds(col, 128)], tiles.at[1], load_sem.at[6]),
        pltpu.make_async_copy(ranks_any.at[1, 0, pl.ds(row, nx), pl.ds(col_back, 128)], tiles.at[2], load_sem.at[7]),
        pltpu.make_async_copy(ranks_any.at[0, 0, pl.ds(row_back, 8), pl.ds(col, 128)], prev, load_sem.at[8]),
        pltpu.make_async_copy(b_any, b, load_sem.at[9]),
    ]
    for load in loads:
        load.start()

    for load in loads[:5]:
        load.wait()
    high, low = halves(binv[...].T)
    wb[0:nz, :] = high
    wb[nz : 2 * nz, :] = high
    wb[2 * nz : 3 * nz, :] = low
    factors = bases[...].reshape(4 * 32, nz)
    high, low = halves(factors.T)
    wc[0:nz, 0:128] = high
    wc[0:nz, 128:256] = low
    wc[nz : 2 * nz, 0:128] = high
    wc[nz : 2 * nz, 128:256] = jnp.zeros((nz, 128), BF16)
    swapped = jnp.concatenate([bases[1], bases[0], bases[3], bases[2]], axis=0)
    high, low = halves(swapped)
    wd[0:128, :] = high
    wd[128:256, :] = high
    wd[256:384, :] = low

    for load in loads[5:9]:
        load.wait()
    lane = lax.broadcasted_iota(jnp.int32, (nx, 128), 1)
    line = lax.broadcasted_iota(jnp.int32, (nx, 128), 0)
    shift = lax.rem(gy, per_tile) * ny
    turned = lambda value, s: pltpu.roll(value, lax.rem(128 + s - shift, 128), 1)
    first, second, second_back = (tiles[k].astype(F32) for k in range(3))
    last = jnp.broadcast_to(prev[...].astype(F32)[7:8, :], (nx, 128))
    before = jnp.where(line == 0, last, pltpu.roll(first, 1, 0))
    seg0 = turned(first, 0)
    seg1 = turned(before, 32)
    seg2 = turned(second, 64)
    seg3 = jnp.where(lane == 96, turned(second_back, 97), turned(second, 97))
    wide[...] = jnp.where(lane < 32, seg0, jnp.where(lane < 64, seg1, jnp.where(lane < 96, seg2, seg3)))
    own = lax.rem(lax.broadcasted_iota(jnp.int32, (ny, 128), 1), 32) == lax.broadcasted_iota(jnp.int32, (ny, 128), 0)
    spread = (
        lax.broadcasted_iota(jnp.int32, (128, 128), 0) // 32 == lax.broadcasted_iota(jnp.int32, (128, 128), 1) // 32
    ).astype(F32).astype(BF16)

    def place(i, _):
        line_ranks = jnp.broadcast_to(wide[pl.ds(i, 1), :], (ny, 128))
        picks[pl.ds(pl.multiple_of(i * ny, ny), ny), :] = jnp.where(own, line_ranks, 0.0).astype(BF16)
        return 0

    lax.fori_loop(0, nx, place, 0, unroll=4)
    step = 16
    rows = step * ny
    level = lax.rem(lax.broadcasted_iota(jnp.int32, (rows, 128), 1), 32).astype(F32)

    def fill_mask(i, _):
        here = pl.ds(pl.multiple_of(i * rows, rows), rows)
        mask[here, :] = jnp.where(level < dot(picks[here, :], spread), 1.0, 0.0)
        return 0

    lax.fori_loop(0, nx // step, fill_mask, 0)

    def cells(x):
        return pl.ds(pl.multiple_of((x + 1) * ny, ny), ny)

    def coefs(c, send):
        def body(i, _):
            here = pl.ds(pl.multiple_of(i * rows, rows), rows)
            both = dot(split[here, :], wc[...])
            both = both[:, :128] + both[:, 128:]
            c[pl.ds(pl.multiple_of(i * rows + ny, ny), rows), :] = both
            first = [both[j * ny : j * ny + 1, :] for j in range(step)]
            last = [both[(j + 1) * ny - 1 : (j + 1) * ny, :] for j in range(step)]
            ends(send, i, first, last)
            return 0

        lax.fori_loop(0, nx // step, body, 0)

    def exchange(k, field, send, recv):
        plan = (
            (field.at[pl.ds(ny, ny), :], field.at[pl.ds((nx + 1) * ny, ny), :], (west, gy)),
            (field.at[pl.ds(nx * ny, ny), :], field.at[pl.ds(0, ny), :], (east, gy)),
            (send.at[0], recv.at[0], (gx, south)),
            (send.at[1], recv.at[1], (gx, north)),
        )
        copies = [
            pltpu.make_async_remote_copy(
                src_ref=src, dst_ref=dst, send_sem=send_sem.at[k, n], recv_sem=recv_sem.at[k, n],
                device_id=to, device_id_type=MESH,
            )
            for n, (src, dst, to) in enumerate(plan)
        ]
        for copy in copies:
            copy.start()
        return copies

    def arrive(copies):
        for copy in copies:
            copy.wait()

    def ends(send, i, first, last):
        here = pl.ds(pl.multiple_of(i * step, step), step)
        send[0, here, :] = jnp.concatenate(first, axis=0)
        send[1, here, :] = jnp.concatenate(last, axis=0)

    def shifted(here, recv, x):
        line = lax.broadcasted_iota(jnp.int32, here.shape, 0)
        after = jnp.broadcast_to(recv[0, pl.ds(x, 1), :], here.shape)
        before = jnp.broadcast_to(recv[1, pl.ds(x, 1), :], here.shape)
        return (
            jnp.where(line == ny - 1, after, pltpu.roll(here, ny - 1, 0)),
            jnp.where(line == 0, before, pltpu.roll(here, 1, 0)),
        )

    def diagonal(write):
        def body(i, _):
            here = pl.ds(pl.multiple_of(i * rows, rows), rows)
            value = split[here, :]
            write(i, dot(jnp.concatenate([value, value[:, :nz]], axis=1), wb[...]))
            return 0

        lax.fori_loop(0, nx // step, body, 0)

    seg = lax.broadcasted_iota(jnp.int32, (ny, 128), 1) // 32

    def couple(c, recv, start, finish):
        def body(i, carry):
            for j in range(step):
                x = i * step + j
                after, before = shifted(c[cells(x), :], recv, x)
                coef = jnp.where(
                    seg == 0, c[cells(x + 1), :], jnp.where(seg == 1, c[cells(x - 1), :], jnp.where(seg == 2, after, before))
                )
                coef = coef * mask[pl.ds(pl.multiple_of(x * ny, ny), ny), :]
                high, low = halves(coef)
                dsplit[j * ny : (j + 1) * ny, 0:128] = high
                dsplit[j * ny : (j + 1) * ny, 128:256] = low
            value = dsplit[...]
            return finish(i, dot(jnp.concatenate([value, value[:, :128]], axis=1), wd[...]), carry)

        return lax.fori_loop(0, nx // step, body, start)

    def put_padded(u):
        def write(i, value):
            u[pl.ds(pl.multiple_of(i * rows + ny, ny), rows), :] = value

        return write

    zero = jnp.zeros((8, nz), F32)

    def operate(u, recv, v, sums):
        def body(x, carry):
            here = u[cells(x), :]
            after, before = shifted(here, recv, x)
            beside = u[cells(x + 1), :] + u[cells(x - 1), :] + after + before
            beside = beside + pltpu.roll(here, 1, 1) + pltpu.roll(here, nz - 1, 1)
            value = (6.0 + mass_shift) * here - beside
            v[x] = value
            at = pl.ds(pl.multiple_of(x * ny, ny), ny)
            high, low = halves(value)
            split[at, 0:nz] = high
            split[at, nz : 2 * nz] = low
            return sums(x, here, value, carry)

        return body

    loads[9].wait()

    def first_split(x, _):
        at = pl.ds(pl.multiple_of(x * ny, ny), ny)
        high, low = halves(b[x])
        split[at, 0:nz] = high
        split[at, nz : 2 * nz] = low
        return 0

    lax.fori_loop(0, nx, first_split, 0, unroll=4)
    coefs(c0, send_c.at[0])
    pl.semaphore_wait(barrier, ndx + ndy - 2)
    copies = exchange(0, c0, send_c.at[0], recv_c.at[0])
    diagonal(put_padded(u0))
    arrive(copies)

    def finish0(i, value, carry):
        first, last = [], []
        for j in range(step):
            x = i * step + j
            total = u0[cells(x), :] + value[j * ny : (j + 1) * ny, :]
            u0[cells(x), :] = total
            first.append(total[:1])
            last.append(total[ny - 1 :])
            carry = carry + fold(total * b[x])
        ends(send_u.at[0], i, first, last)
        return carry

    bu0 = couple(c0, recv_c.at[0], zero, finish0)

    copies = exchange(1, u0, send_u.at[0], recv_u.at[0])
    arrive(copies)
    body = operate(u0, recv_u.at[0], v0, lambda x, here, value, carry: carry + fold(here * value))
    u0v0 = lax.fori_loop(0, nx, body, zero, unroll=2)

    coefs(c1, send_c.at[1])
    copies = exchange(2, c1, send_c.at[1], recv_c.at[1])
    diagonal(put_padded(u1))
    arrive(copies)

    def finish1(i, value, carry):
        one, two = carry
        first, last = [], []
        for j in range(step):
            x = i * step + j
            total = u1[cells(x), :] + value[j * ny : (j + 1) * ny, :]
            u1[cells(x), :] = total
            first.append(total[:1])
            last.append(total[ny - 1 :])
            one = one + fold(total * b[x])
            two = two + fold(total * v0[x])
        ends(send_u.at[1], i, first, last)
        return one, two

    bu1, v0u1 = couple(c1, recv_c.at[1], (zero, zero), finish1)

    copies = exchange(3, u1, send_u.at[1], recv_u.at[1])
    arrive(copies)
    body = operate(u1, recv_u.at[1], v1, lambda x, here, value, carry: carry + fold(here * value))
    u1v1 = lax.fori_loop(0, nx, body, zero, unroll=2)

    def lines(value):
        value = value[:, :128] + value[:, 128:]
        return jnp.sum(value, axis=0, keepdims=True)

    partial = jnp.concatenate(
        [lines(s) for s in (bu0, u0v0, bu1, v0u1, u1v1)] + [jnp.zeros((3, 128), F32)], axis=0
    )
    part[0] = partial
    got_y[gy] = partial
    along_y = [
        pltpu.make_async_remote_copy(
            src_ref=part.at[0], dst_ref=got_y.at[gy], send_sem=rsend_sem.at[0, k], recv_sem=rrecv_sem.at[0, k],
            device_id=(gx, lax.rem(gy + k, ndy)), device_id_type=MESH,
        )
        for k in range(1, ndy)
    ]
    for copy in along_y:
        copy.start()

    coefs(c2, send_c.at[2])
    copies = exchange(4, c2, send_c.at[2], recv_c.at[2])
    for copy in along_y:
        copy.wait()
    partial = jnp.sum(got_y[...], axis=0)
    part[1] = partial
    got_x[gx] = partial
    along_x = [
        pltpu.make_async_remote_copy(
            src_ref=part.at[1], dst_ref=got_x.at[gx], send_sem=rsend_sem.at[1, k], recv_sem=rrecv_sem.at[1, k],
            device_id=(lax.rem(gx + k, ndx), gy), device_id_type=MESH,
        )
        for k in range(1, ndx)
    ]
    for copy in along_x:
        copy.start()

    def write_u2(i, value):
        u2[pl.ds(pl.multiple_of(i * rows, rows), rows), :] = value

    diagonal(write_u2)
    arrive(copies)

    def finish2(i, value, carry):
        here = pl.ds(pl.multiple_of(i * rows, rows), rows)
        u2[here, :] = u2[here, :] + value
        return carry

    couple(c2, recv_c.at[2], 0, finish2)

    for copy in along_x:
        copy.wait()
    total = jnp.sum(jnp.sum(got_x[...], axis=0), axis=1, keepdims=True)
    s = [total[k : k + 1, :] for k in range(5)]

    alpha0 = s[S_BU0] / s[S_U0V0]
    rz1 = s[S_BU0] - alpha0 * (s[S_U0V0] + s[S_BU1]) + alpha0 * (alpha0 * s[S_V0U1])
    grow = 1.0 + rz1 / s[S_BU0]
    curve = grow * (grow * s[S_U0V0] - 2.0 * (alpha0 * s[S_V0U1])) + alpha0 * (alpha0 * s[S_U1V1])
    alpha1 = rz1 / curve
    on0 = alpha0 + alpha1 * grow
    on1 = -(alpha1 * alpha0)
    on0 = jnp.broadcast_to(on0, (ny, nz))
    on1 = jnp.broadcast_to(on1, (ny, nz))

    def final(x, _):
        at = pl.ds(pl.multiple_of(x * ny, ny), ny)
        f0, f1 = u0[cells(x), :], u1[cells(x), :]
        x_out[x] = on0 * f0 + on1 * f1
        gap_out[x] = b[x] - on0 * v0[x] - on1 * v1[x]
        z_out[x] = f0 - on0 * f1 - on1 * u2[at, :]
        return 0

    lax.fori_loop(0, nx, final, 0, unroll=2)


def per_device(devs, right_side, block_inverse, basis_left, basis_right, ranks):
    nx, ny, nz = right_side.shape
    ndx, ndy = devs
    lines = nx * ny
    padded = lines + 2 * ny
    out = jax.ShapeDtypeStruct(right_side.shape, F32)
    return pl.pallas_call(
        functools.partial(kernel, devs),
        out_shape=(out, out, out),
        in_specs=[pl.BlockSpec(memory_space=pl.ANY)] * 5,
        out_specs=[pl.BlockSpec(memory_space=pltpu.VMEM)] * 3,
        scratch_shapes=[
            pltpu.VMEM((nx, ny, nz), F32),
            pltpu.VMEM((nz, nz), F32),
            pltpu.VMEM((4, 32, nz), F32),
            pltpu.VMEM((3, nx, 128), jnp.int32),
            pltpu.VMEM((8, 128), jnp.int32),
            pltpu.VMEM((nx, 128), F32),
            pltpu.VMEM((3 * nz, nz), BF16),
            pltpu.VMEM((2 * nz, 256), BF16),
            pltpu.VMEM((384, nz), BF16),
            pltpu.VMEM((lines, 128), BF16),
            pltpu.VMEM((lines, 128), F32),
            pltpu.VMEM((lines, 2 * nz), BF16),
            pltpu.VMEM((16 * ny, 256), BF16),
            pltpu.VMEM((padded, nz), F32),
            pltpu.VMEM((padded, nz), F32),
            pltpu.VMEM((lines, nz), F32),
            pltpu.VMEM((nx, ny, nz), F32),
            pltpu.VMEM((nx, ny, nz), F32),
            pltpu.VMEM((padded, 128), F32),
            pltpu.VMEM((padded, 128), F32),
            pltpu.VMEM((padded, 128), F32),
            pltpu.VMEM((3, 2, nx, 128), F32),
            pltpu.VMEM((3, 2, nx, 128), F32),
            pltpu.VMEM((2, 2, nx, nz), F32),
            pltpu.VMEM((2, 2, nx, nz), F32),
            pltpu.VMEM((2, 8, 128), F32),
            pltpu.VMEM((ndy, 8, 128), F32),
            pltpu.VMEM((ndx, 8, 128), F32),
            pltpu.SemaphoreType.DMA((10,)),
            pltpu.SemaphoreType.DMA((5, 4)),
            pltpu.SemaphoreType.DMA((5, 4)),
            pltpu.SemaphoreType.DMA((2, ndy)),
            pltpu.SemaphoreType.DMA((2, ndy)),
        ],
        compiler_params=pltpu.CompilerParams(
            collective_id=0, has_side_effects=True, vmem_limit_bytes=48 * 1024 * 1024
        ),
    )(right_side, block_inverse, basis_left, basis_right, ranks)


def solution(mesh):
    devs = (mesh.shape["gx"], mesh.shape["gy"])
    return jax.shard_map(
        functools.partial(per_device, devs),
        mesh=mesh,
        in_specs=(P("gx", "gy", None), P(), P(), P(), P()),
        out_specs=(P("gx", "gy", None),) * 3,
        check_vma=False,
    )
```

profile of v0, /device:TPU:0, one launch (start us, length us, event | category | flops | bytes accessed | tf_op | source)
XLA Modules:
  0.0 58.9 jit_solution(16300971831257915196)
XLA Ops:
  0.6 0.0 copy-start
  0.6 0.9 %copy-done = f32[1,256,256]{2,1,0:T(8,128)S(1)} copy-done((f32[1,256,256]{2,1,0:T(8,128)S(1)}, f32[1,256,256]{2,1,0:T(8,128)}, u32[]{:S(2)}) %copy-start) | copy-done | bytes 262168
  1.6 0.0 copy-start.1
  1.6 0.8 %copy-done.1 = f32[2,1,32,256]{3,2,1,0:T(8,128)S(1)} copy-done((f32[2,1,32,256]{3,2,1,0:T(8,128)S(1)}, f32[2,1,32,256]{3,2,1,0:T(8,128)}, u32[]{:S(2)}) %copy-start.1) | copy-done | bytes 65560
  2.4 0.0 copy-start.2
  2.4 0.8 %copy-done.2 = f32[2,1,32,256]{3,2,1,0:T(8,128)S(1)} copy-done((f32[2,1,32,256]{3,2,1,0:T(8,128)S(1)}, f32[2,1,32,256]{3,2,1,0:T(8,128)}, u32[]{:S(2)}) %copy-start.2) | copy-done | bytes 65560
  3.3 50.6 %shard_map.76 = (f32[64,32,256]{2,1,0:T(8,128)S(1)}, f32[64,32,256]{2,1,0:T(8,128)S(1)}, f32[64,32,256]{2,1,0:T(8,128)}) custom-call(f32[64,32,256]{2,1,0:T(8,128)} %b_any.1, f32[1,256,256]{2,1,0:T(8,128)S(1)} %copy-done, f32[2,1,32,256]{3,2,1,0:T(8,128)S(1)} %copy-done.1, f32[2,1,32,256]{3,2,1,0:T(8,128)S(1)} %copy-done.2, s32[2,1,512,512]{3,2,1,0:T(8,128)} %ranks_any.1), custom_call_target="tpu_custom_call" | custom-call | tf_op jit(solution)/shard_map/pallas_call | solution.py:374
  53.9 1.3 %copy.11 = f32[64,32,256]{2,1,0:T(8,128)} copy(f32[64,32,256]{2,1,0:T(8,128)S(1)} %get-tuple-element.6) | data formatting | bytes 4194304
  55.2 0.0 copy-start.3
  55.2 1.3 %copy.12 = f32[64,32,256]{2,1,0:T(8,128)} copy(f32[64,32,256]{2,1,0:T(8,128)S(1)} %get-tuple-element.7) | data formatting | bytes 4194304
  56.5 1.0 %copy-done.3 = f32[64,32,256]{2,1,0:T(8,128)S(1)} copy-done((f32[64,32,256]{2,1,0:T(8,128)S(1)}, f32[64,32,256]{2,1,0:T(8,128)}, u32[]{:S(2)}) %copy-start.3) | copy-done | bytes 2097176
  57.6 1.3 %copy.13 = f32[64,32,256]{2,1,0:T(8,128)} copy(f32[64,32,256]{2,1,0:T(8,128)S(1)} %copy-done.3) | data formatting | bytes 4194304
Async XLA Ops:
  0.6 1.0 %copy-start = (f32[1,256,256]{2,1,0:T(8,128)S(1)}, f32[1,256,256]{2,1,0:T(8,128)}, u32[]{:S(2)}) copy-start(f32[1,256,256]{2,1,0:T(8,128)} %binv_any.1) | copy-start | bytes 786436
  1.6 0.8 %copy-start.1 = (f32[2,1,32,256]{3,2,1,0:T(8,128)S(1)}, f32[2,1,32,256]{3,2,1,0:T(8,128)}, u32[]{:S(2)}) copy-start(f32[2,1,32,256]{3,2,1,0:T(8,128)} %left_any.1) | copy-start | bytes 196612
  2.4 0.8 %copy-start.2 = (f32[2,1,32,256]{3,2,1,0:T(8,128)S(1)}, f32[2,1,32,256]{3,2,1,0:T(8,128)}, u32[]{:S(2)}) copy-start(f32[2,1,32,256]{3,2,1,0:T(8,128)} %right_any.1) | copy-start | bytes 196612
  55.2 2.3 %copy-start.3 = (f32[64,32,256]{2,1,0:T(8,128)S(1)}, f32[64,32,256]{2,1,0:T(8,128)}, u32[]{:S(2)}) copy-start(f32[64,32,256]{2,1,0:T(8,128)} %get-tuple-element.8) | copy-start | bytes 6291460
where the time goes:
time: 59.6 us; the launch traced here: 58.9 us
  Pallas kernels  50.6 us (85%)
  local copies, waits for them, and re-layouts  7.61 us (13%)
  between operations  0.65 us (1%)
    pallas_call x1, Pallas kernels, per_device(): pl.pallas_call(functools.partial(kernel, devs), out_shape=(out, out, out)...  50.6 us
    unnamed x11, local copies, waits for them, and re-layouts  7.61 us

commit v1 on v0

--- a/solution.py
+++ b/solution.py
@@ -32,11 +32,11 @@
 
 def kernel(
     devs, b_any, binv_any, left_any, right_any, ranks_any,
-    x_out, gap_out, z_out,
-    b, binv, bases, tiles, prev, wide, wb, wc, wd, picks, mask, split, dsplit,
-    u0, u1, u2, v0, v1, c0, c1, c2,
+    b, u0, u1, u2, v0, v1, scale,
+    binv, bases, tiles, prev, wide, wb, wc, wd, picks, mask, split, dsplit,
+    c0, c1, c2,
     send_c, recv_c, send_u, recv_u, part, got_y, got_x,
-    load_sem, send_sem, recv_sem, rsend_sem, rrecv_sem,
+    load_sem, xsend_sem, xrecv_sem, ysend_sem, yrecv_sem, rsend_sem, rrecv_sem,
 ):
     ndx, ndy = devs
     nx, ny, nz = b.shape
@@ -125,48 +125,87 @@
 
     lax.fori_loop(0, nx // step, fill_mask, 0)
 
+    chunks = nx // step
+
+    def chunk(i):
+        return jnp.where(i == 0, 0, jnp.where(i == 1, chunks - 1, i - 1))
+
     def cells(x):
         return pl.ds(pl.multiple_of((x + 1) * ny, ny), ny)
 
-    def coefs(c, send):
-        def body(i, _):
-            here = pl.ds(pl.multiple_of(i * rows, rows), rows)
-            both = dot(split[here, :], wc[...])
-            both = both[:, :128] + both[:, 128:]
-            c[pl.ds(pl.multiple_of(i * rows + ny, ny), rows), :] = both
-            first = [both[j * ny : j * ny + 1, :] for j in range(step)]
-            last = [both[(j + 1) * ny - 1 : (j + 1) * ny, :] for j in range(step)]
-            ends(send, i, first, last)
-            return 0
-
-        lax.fori_loop(0, nx // step, body, 0)
-
-    def exchange(k, field, send, recv):
-        plan = (
-            (field.at[pl.ds(ny, ny), :], field.at[pl.ds((nx + 1) * ny, ny), :], (west, gy)),
-            (field.at[pl.ds(nx * ny, ny), :], field.at[pl.ds(0, ny), :], (east, gy)),
-            (send.at[0], recv.at[0], (gx, south)),
-            (send.at[1], recv.at[1], (gx, north)),
+    def flat(i):
+        return pl.ds(pl.multiple_of(i * rows, rows), rows)
+
+    def inner(i):
+        return pl.ds(pl.multiple_of(i * rows + ny, ny), rows)
+
+    class Halo:
+        def __init__(self, k, field, send, recv):
+            self.k, self.field, self.send, self.recv = k, field, send, recv
+
+        def x_copy(self, side):
+            mine, theirs, to = ((ny, (nx + 1) * ny, west), (nx * ny, 0, east))[side]
+            return pltpu.make_async_remote_copy(
+                src_ref=self.field.at[pl.ds(mine, ny), :], dst_ref=self.field.at[pl.ds(theirs, ny), :],
+                send_sem=xsend_sem.at[self.k, side], recv_sem=xrecv_sem.at[self.k, side],
+                device_id=(to, gy), device_id_type=MESH,
+            )
+
+        def y_copy(self, side, i):
+            here = pl.ds(pl.multiple_of(i * step, step), step)
+            return pltpu.make_async_remote_copy(
+                src_ref=self.send.at[side, here, :], dst_ref=self.recv.at[side, here, :],
+                send_sem=ysend_sem.at[self.k, side, i], recv_sem=yrecv_sem.at[self.k, side, i],
+                device_id=(gx, (south, north)[side]), device_id_type=MESH,
+            )
+
+        def store_ends(self, i, first, last):
+            here = pl.ds(pl.multiple_of(i * step, step), step)
+            self.send[0, here, :] = jnp.concatenate(first, axis=0)
+            self.send[1, here, :] = jnp.concatenate(last, axis=0)
+
+        def start(self, turn, i):
+            @pl.when(turn == 0)
+            def _():
+                self.x_copy(0).start()
+
+            @pl.when(turn == 1)
+            def _():
+                self.x_copy(1).start()
+
+            for side in (0, 1):
+                self.y_copy(side, i).start()
+
+        def arrive(self, turn, i):
+            @pl.when(turn == 0)
+            def _():
+                self.x_copy(1).wait_recv()
+
+            @pl.when(turn == 1)
+            def _():
+                self.x_copy(0).wait_recv()
+
+            for side in (0, 1):
+                self.y_copy(side, i).wait_recv()
+
+        def drain(self):
+            for side in (0, 1):
+                self.x_copy(side).wait_send()
+                for i in range(chunks):
+                    self.y_copy(side, i).wait_send()
+
+    cs = [Halo(k, c, send_c.at[k], recv_c.at[k]) for k, c in enumerate((c0, c1, c2))]
+    us = [Halo(3 + k, u, send_u.at[k], recv_u.at[k]) for k, u in enumerate((u0, u1))]
+
+    def coefs(halo, i):
+        both = dot(split[flat(i), :], wc[...])
+        both = both[:, :128] + both[:, 128:]
+        halo.field[inner(i), :] = both
+        halo.store_ends(
+            i,
+            [both[j * ny : j * ny + 1, :] for j in range(step)],
+            [both[(j + 1) * ny - 1 : (j + 1) * ny, :] for j in range(step)],
         )
-        copies = [
-            pltpu.make_async_remote_copy(
-                src_ref=src, dst_ref=dst, send_sem=send_sem.at[k, n], recv_sem=recv_sem.at[k, n],
-                device_id=to, device_id_type=MESH,
-            )
-            for n, (src, dst, to) in enumerate(plan)
-        ]
-        for copy in copies:
-            copy.start()
-        return copies
-
-    def arrive(copies):
-        for copy in copies:
-            copy.wait()
-
-    def ends(send, i, first, last):
-        here = pl.ds(pl.multiple_of(i * step, step), step)
-        send[0, here, :] = jnp.concatenate(first, axis=0)
-        send[1, here, :] = jnp.concatenate(last, axis=0)
 
     def shifted(here, recv, x):
         line = lax.broadcasted_iota(jnp.int32, here.shape, 0)
@@ -177,19 +216,22 @@
             jnp.where(line == 0, before, pltpu.roll(here, 1, 0)),
         )
 
-    def diagonal(write):
+    def diagonal(out, place):
         def body(i, _):
-            here = pl.ds(pl.multiple_of(i * rows, rows), rows)
-            value = split[here, :]
-            write(i, dot(jnp.concatenate([value, value[:, :nz]], axis=1), wb[...]))
+            value = split[flat(i), :]
+            out[place(i), :] = dot(jnp.concatenate([value, value[:, :nz]], axis=1), wb[...])
             return 0
 
-        lax.fori_loop(0, nx // step, body, 0)
+        lax.fori_loop(0, chunks, body, 0)
 
     seg = lax.broadcasted_iota(jnp.int32, (ny, 128), 1) // 32
 
-    def couple(c, recv, start, finish):
-        def body(i, carry):
+    def couple(halo, start, finish):
+        c, recv = halo.field, halo.recv
+
+        def body(turn, carry):
+            i = chunk(turn)
+            halo.arrive(turn, i)
             for j in range(step):
                 x = i * step + j
                 after, before = shifted(c[cells(x), :], recv, x)
@@ -201,33 +243,57 @@
                 dsplit[j * ny : (j + 1) * ny, 0:128] = high
                 dsplit[j * ny : (j + 1) * ny, 128:256] = low
             value = dsplit[...]
-            return finish(i, dot(jnp.concatenate([value, value[:, :128]], axis=1), wd[...]), carry)
-
-        return lax.fori_loop(0, nx // step, body, start)
-
-    def put_padded(u):
-        def write(i, value):
-            u[pl.ds(pl.multiple_of(i * rows + ny, ny), rows), :] = value
-
-        return write
+            return finish(turn, i, dot(jnp.concatenate([value, value[:, :128]], axis=1), wd[...]), carry)
+
+        return lax.fori_loop(0, chunks, body, start)
 
     zero = jnp.zeros((8, nz), F32)
 
-    def operate(u, recv, v, sums):
-        def body(x, carry):
-            here = u[cells(x), :]
-            after, before = shifted(here, recv, x)
-            beside = u[cells(x + 1), :] + u[cells(x - 1), :] + after + before
-            beside = beside + pltpu.roll(here, 1, 1) + pltpu.roll(here, nz - 1, 1)
-            value = (6.0 + mass_shift) * here - beside
-            v[x] = value
-            at = pl.ds(pl.multiple_of(x * ny, ny), ny)
-            high, low = halves(value)
-            split[at, 0:nz] = high
-            split[at, nz : 2 * nz] = low
-            return sums(x, here, value, carry)
-
-        return body
+    def finish_field(halo, sums):
+        u = halo.field
+
+        def finish(turn, i, value, carry):
+            first, last = [], []
+            for j in range(step):
+                x = i * step + j
+                total = u[cells(x), :] + value[j * ny : (j + 1) * ny, :]
+                u[cells(x), :] = total
+                first.append(total[:1])
+                last.append(total[ny - 1 :])
+                carry = sums(x, total, carry)
+            halo.store_ends(i, first, last)
+            halo.start(turn, i)
+            return carry
+
+        return finish
+
+    def operate(halo, v, next_halo):
+        u, recv = halo.field, halo.recv
+
+        def body(turn, carry):
+            i = chunk(turn)
+            halo.arrive(turn, i)
+
+            def line(j, carry):
+                x = i * step + j
+                here = u[cells(x), :]
+                after, before = shifted(here, recv, x)
+                beside = u[cells(x + 1), :] + u[cells(x - 1), :] + after + before
+                beside = beside + pltpu.roll(here, 1, 1) + pltpu.roll(here, nz - 1, 1)
+                value = (6.0 + mass_shift) * here - beside
+                v[x] = value
+                at = pl.ds(pl.multiple_of(x * ny, ny), ny)
+                high, low = halves(value)
+                split[at, 0:nz] = high
+                split[at, nz : 2 * nz] = low
+                return carry + fold(here * value)
+
+            carry = lax.fori_loop(0, step, line, carry, unroll=4)
+            coefs(next_halo, i)
+            next_halo.start(turn, i)
+            return carry
+
+        return lax.fori_loop(0, chunks, body, zero)
 
     loads[9].wait()
 
@@ -239,56 +305,32 @@
         return 0
 
     lax.fori_loop(0, nx, first_split, 0, unroll=4)
-    coefs(c0, send_c.at[0])
+
+    def first_coefs(i, _):
+        coefs(cs[0], i)
+        return 0
+
+    lax.fori_loop(0, chunks, first_coefs, 0)
+    diagonal(u0, inner)
     pl.semaphore_wait(barrier, ndx + ndy - 2)
-    copies = exchange(0, c0, send_c.at[0], recv_c.at[0])
-    diagonal(put_padded(u0))
-    arrive(copies)
-
-    def finish0(i, value, carry):
-        first, last = [], []
-        for j in range(step):
-            x = i * step + j
-            total = u0[cells(x), :] + value[j * ny : (j + 1) * ny, :]
-            u0[cells(x), :] = total
-            first.append(total[:1])
-            last.append(total[ny - 1 :])
-            carry = carry + fold(total * b[x])
-        ends(send_u.at[0], i, first, last)
-        return carry
-
-    bu0 = couple(c0, recv_c.at[0], zero, finish0)
-
-    copies = exchange(1, u0, send_u.at[0], recv_u.at[0])
-    arrive(copies)
-    body = operate(u0, recv_u.at[0], v0, lambda x, here, value, carry: carry + fold(here * value))
-    u0v0 = lax.fori_loop(0, nx, body, zero, unroll=2)
-
-    coefs(c1, send_c.at[1])
-    copies = exchange(2, c1, send_c.at[1], recv_c.at[1])
-    diagonal(put_padded(u1))
-    arrive(copies)
-
-    def finish1(i, value, carry):
-        one, two = carry
-        first, last = [], []
-        for j in range(step):
-            x = i * step + j
-            total = u1[cells(x), :] + value[j * ny : (j + 1) * ny, :]
-            u1[cells(x), :] = total
-            first.append(total[:1])
-            last.append(total[ny - 1 :])
-            one = one + fold(total * b[x])
-            two = two + fold(total * v0[x])
-        ends(send_u.at[1], i, first, last)
-        return one, two
-
-    bu1, v0u1 = couple(c1, recv_c.at[1], (zero, zero), finish1)
-
-    copies = exchange(3, u1, send_u.at[1], recv_u.at[1])
-    arrive(copies)
-    body = operate(u1, recv_u.at[1], v1, lambda x, here, value, carry: carry + fold(here * value))
-    u1v1 = lax.fori_loop(0, nx, body, zero, unroll=2)
+
+    def first_start(turn, _):
+        cs[0].start(turn, chunk(turn))
+        return 0
+
+    lax.fori_loop(0, chunks, first_start, 0)
+    bu0 = couple(cs[0], zero, finish_field(us[0], lambda x, total, carry: carry + fold(total * b[x])))
+
+    u0v0 = operate(us[0], v0, cs[1])
+
+    diagonal(u1, inner)
+    bu1, v0u1 = couple(
+        cs[1],
+        (zero, zero),
+        finish_field(us[1], lambda x, total, carry: (carry[0] + fold(total * b[x]), carry[1] + fold(total * v0[x]))),
+    )
+
+    u1v1 = operate(us[1], v1, cs[2])
 
     def lines(value):
         value = value[:, :128] + value[:, 128:]
@@ -309,8 +351,7 @@
     for copy in along_y:
         copy.start()
 
-    coefs(c2, send_c.at[2])
-    copies = exchange(4, c2, send_c.at[2], recv_c.at[2])
+    diagonal(u2, flat)
     for copy in along_y:
         copy.wait()
     partial = jnp.sum(got_y[...], axis=0)
@@ -326,19 +367,13 @@
     for copy in along_x:
         copy.start()
 
-    def write_u2(i, value):
-        u2[pl.ds(pl.multiple_of(i * rows, rows), rows), :] = value
-
-    diagonal(write_u2)
-    arrive(copies)
-
-    def finish2(i, value, carry):
-        here = pl.ds(pl.multiple_of(i * rows, rows), rows)
-        u2[here, :] = u2[here, :] + value
+    def finish2(turn, i, value, carry):
+        u2[flat(i), :] = u2[flat(i), :] + value
         return carry
 
-    couple(c2, recv_c.at[2], 0, finish2)
-
+    couple(cs[2], 0, finish2)
+    for halo in cs + us:
+        halo.drain()
     for copy in along_x:
         copy.wait()
     total = jnp.sum(jnp.sum(got_x[...], axis=0), axis=1, keepdims=True)
@@ -351,18 +386,42 @@
     alpha1 = rz1 / curve
     on0 = alpha0 + alpha1 * grow
     on1 = -(alpha1 * alpha0)
-    on0 = jnp.broadcast_to(on0, (ny, nz))
-    on1 = jnp.broadcast_to(on1, (ny, nz))
-
-    def final(x, _):
-        at = pl.ds(pl.multiple_of(x * ny, ny), ny)
-        f0, f1 = u0[cells(x), :], u1[cells(x), :]
-        x_out[x] = on0 * f0 + on1 * f1
-        gap_out[x] = b[x] - on0 * v0[x] - on1 * v1[x]
-        z_out[x] = f0 - on0 * f1 - on1 * u2[at, :]
-        return 0
-
-    lax.fori_loop(0, nx, final, 0, unroll=2)
+    scale[0] = jnp.broadcast_to(on0, (8, 128))
+    scale[1] = jnp.broadcast_to(on1, (8, 128))
+
+
+def combine(b, u0, u1, u2, v0, v1, scale, x_any, gap_any, z_any, x_out, gap_out, z_out, sem):
+    nx, ny, nz = x_out.shape
+    step = 8
+    on0, on1 = (jnp.concatenate([jnp.concatenate([scale[k]] * 2, axis=1)] * (ny // 8), axis=0) for k in (0, 1))
+
+    def copies(i):
+        here = pl.ds(pl.multiple_of(i * step, step), step)
+        return [
+            pltpu.make_async_copy(out.at[here], out_any.at[here], sem.at[n, i])
+            for n, (out, out_any) in enumerate(((x_out, x_any), (z_out, z_any), (gap_out, gap_any)))
+        ]
+
+    def body(i, _):
+        for j in range(step):
+            x = i * step + j
+            at = pl.ds(pl.multiple_of((x + 1) * ny, ny), ny)
+            f0, f1 = u0[at, :], u1[at, :]
+            x_out[x] = on0 * f0 + on1 * f1
+            z_out[x] = f0 - on0 * f1 - on1 * u2[pl.ds(pl.multiple_of(x * ny, ny), ny), :]
+            gap_out[x] = b[x] - on0 * v0[x] - on1 * v1[x]
+        for copy in copies(i):
+            copy.start()
+        return 0
+
+    lax.fori_loop(0, nx // step, body, 0)
+
+    def finish(i, _):
+        for copy in copies(i):
+            copy.wait()
+        return 0
+
+    lax.fori_loop(0, nx // step, finish, 0)
 
 
 def per_device(devs, right_side, block_inverse, basis_left, basis_right, ranks):
@@ -370,14 +429,18 @@
     ndx, ndy = devs
     lines = nx * ny
     padded = lines + 2 * ny
-    out = jax.ShapeDtypeStruct(right_side.shape, F32)
-    return pl.pallas_call(
+    block = jax.ShapeDtypeStruct(right_side.shape, F32)
+    framed = jax.ShapeDtypeStruct((padded, nz), F32)
+    arrays = (right_side, block_inverse, basis_left, basis_right, ranks)
+    fields = pl.pallas_call(
         functools.partial(kernel, devs),
-        out_shape=(out, out, out),
-        in_specs=[pl.BlockSpec(memory_space=pl.ANY)] * 5,
-        out_specs=[pl.BlockSpec(memory_space=pltpu.VMEM)] * 3,
+        out_shape=(
+            block, framed, framed, jax.ShapeDtypeStruct((lines, nz), F32), block, block,
+            jax.ShapeDtypeStruct((2, 8, 128), F32),
+        ),
+        in_specs=[pl.BlockSpec(memory_space=pltpu.HBM)] * 5,
+        out_specs=[pl.BlockSpec(memory_space=pltpu.VMEM)] * 7,
         scratch_shapes=[
-            pltpu.VMEM((nx, ny, nz), F32),
             pltpu.VMEM((nz, nz), F32),
             pltpu.VMEM((4, 32, nz), F32),
             pltpu.VMEM((3, nx, 128), jnp.int32),
@@ -390,11 +453,6 @@
             pltpu.VMEM((lines, 128), F32),
             pltpu.VMEM((lines, 2 * nz), BF16),
             pltpu.VMEM((16 * ny, 256), BF16),
-            pltpu.VMEM((padded, nz), F32),
-            pltpu.VMEM((padded, nz), F32),
-            pltpu.VMEM((lines, nz), F32),
-            pltpu.VMEM((nx, ny, nz), F32),
-            pltpu.VMEM((nx, ny, nz), F32),
             pltpu.VMEM((padded, 128), F32),
             pltpu.VMEM((padded, 128), F32),
             pltpu.VMEM((padded, 128), F32),
@@ -406,15 +464,25 @@
             pltpu.VMEM((ndy, 8, 128), F32),
             pltpu.VMEM((ndx, 8, 128), F32),
             pltpu.SemaphoreType.DMA((10,)),
-            pltpu.SemaphoreType.DMA((5, 4)),
-            pltpu.SemaphoreType.DMA((5, 4)),
+            pltpu.SemaphoreType.DMA((5, 2)),
+            pltpu.SemaphoreType.DMA((5, 2)),
+            pltpu.SemaphoreType.DMA((5, 2, nx // 16)),
+            pltpu.SemaphoreType.DMA((5, 2, nx // 16)),
             pltpu.SemaphoreType.DMA((2, ndy)),
             pltpu.SemaphoreType.DMA((2, ndy)),
         ],
         compiler_params=pltpu.CompilerParams(
-            collective_id=0, has_side_effects=True, vmem_limit_bytes=48 * 1024 * 1024
+            collective_id=0, has_side_effects=True, vmem_limit_bytes=32 * 1024 * 1024
         ),
-    )(right_side, block_inverse, basis_left, basis_right, ranks)
+    )(*(pltpu.with_memory_space_constraint(array, pltpu.HBM) for array in arrays))
+    return pl.pallas_call(
+        combine,
+        out_shape=(block, block, block),
+        in_specs=[pl.BlockSpec(memory_space=pltpu.VMEM)] * 7,
+        out_specs=[pl.BlockSpec(memory_space=pltpu.HBM)] * 3,
+        scratch_shapes=[pltpu.VMEM((nx, ny, nz), F32)] * 3 + [pltpu.SemaphoreType.DMA((3, nx // 8))],
+        compiler_params=pltpu.CompilerParams(vmem_limit_bytes=32 * 1024 * 1024),
+    )(*fields)
 
 
 def solution(mesh):

time: 59.6 us -> 45.9 us (0.77)
  local copies, waits for them, and re-layouts: 7.61 us -> 0 us
  Pallas kernels: 50.6 us -> 45 us
    unnamed x11 -> x0, local copies, waits for them, and re-layouts: 7.61 us -> none
    pallas_call x1 -> x2, Pallas kernels: 50.6 us -> 45 us  [the longest x1 42.1 us: per_device(): pl.pallas_call(functools.partial(kernel, devs), out_shape=(block, framed,...]
where the time goes in v1:
time: 45.9 us; the launch traced here: 45.6 us
  Pallas kernels  45 us (98%)
  between operations  0.64 us (1%)
    pallas_call x1, Pallas kernels, per_device(): pl.pallas_call(functools.partial(kernel, devs), out_shape=(block, framed,...  42.1 us
    pallas_call x1, Pallas kernels, per_device(): pl.pallas_call(combine, out_shape=(block, block, block), in_specs=[pl.Blo...  2.89 us

profile of v1, /device:TPU:0, one launch (start us, length us, event | category | flops | bytes accessed | tf_op | source)
XLA Modules:
  0.0 45.6 jit_solution(4961617704662078391)
XLA Ops:
  0.6 42.1 %shard_map.76 = (f32[64,32,256]{2,1,0:T(8,128)S(1)}, f32[2112,256]{1,0:T(8,128)S(1)}, f32[2112,256]{1,0:T(8,128)S(1)}, f32[2048,256]{1,0:T(8,128)S(1)}, f32[64,3...) custom-call(f32[64,32,256]{2,1,0:T(8,128)} %b_any.1, f32[1,256,256]{2,1,0:T(8,128)} %binv_any.1, ...), custom_call_target="tpu_custom_call" | custom-call | tf_op jit(solution)/shard_map/pallas_call | solution.py:435
  42.8 2.9 %shard_map.77 = (f32[64,32,256]{2,1,0:T(8,128)}, f32[64,32,256]{2,1,0:T(8,128)}, f32[64,32,256]{2,1,0:T(8,128)}) custom-call(f32[64,32,256]{2,1,0:T(8,128)S(1)} %get-tuple-element.10.b, f32[2112,256]{1,0:T(8,128)S(1)} %get-tuple-element.11.u0, f32[2112,256]{1,0:T(8,128)S(1)} %get-tuple-element.12.u1, f32[2048,256]{1,0:T(8,128)S(1)} %get-tuple-element.13.u2, ...), custom_call_target="tpu_custom_call" | custom-call | tf_op jit(solution)/shard_map/pallas_call | solution.py:478

commit v2 on v1

v2 whole, which is shorter than its diff:
```python
import functools

import jax
import jax.numpy as jnp
from jax import lax
from jax.experimental import pallas as pl
from jax.experimental.pallas import tpu as pltpu
from jax.sharding import PartitionSpec as P

F32 = jnp.float32
BF16 = jnp.bfloat16
MESH = pl.DeviceIdType.MESH

mass_shift = 0.05

S_BU0, S_U0V0, S_BU1, S_V0U1, S_U1V1 = range(5)


def halves(value):
    high = value.astype(BF16)
    return high, (value - high.astype(F32)).astype(BF16)


def dot(a, b):
    return lax.dot_general(a, b, (((1,), (0,)), ((), ())), preferred_element_type=F32)


def fold(value):
    rows, width = value.shape
    return jnp.sum(value.reshape(rows // 8, 8, width), axis=0)


def kernel(
    devs, b_any, binv_any, left_any, right_any, ranks_any,
    b, u0, u1, u2, v0, v1, scale,
    binv, bases, tiles, limits, picks, wb, wc, wd, mask, edge_mask, split, dsplit, fsplit,
    c, coef_send, coef_recv, raw_send, raw_recv, corner_send, corner_recv, uy, part, got_y, got_x,
    load_sem, xsend_sem, xrecv_sem, ysend_sem, yrecv_sem, ksend_sem, krecv_sem, rsend_sem, rrecv_sem,
):
    ndx, ndy = devs
    nx, ny, nz = b.shape
    lines = nx * ny
    edge = 2 * ny + 2 * nx
    step = 16
    rows = step * ny
    chunks = nx // step
    gx = lax.axis_index("gx")
    gy = lax.axis_index("gy")
    east, west = lax.rem(gx + 1, ndx), lax.rem(gx + ndx - 1, ndx)
    north, south = lax.rem(gy + 1, ndy), lax.rem(gy + ndy - 1, ndy)
    diagonals = ((east, north), (east, south), (west, north), (west, south))

    barrier = pltpu.get_barrier_semaphore()
    for k in range(1, ndy):
        pl.semaphore_signal(barrier, 1, device_id=(gx, lax.rem(gy + k, ndy)), device_id_type=MESH)
    for k in range(1, ndx):
        pl.semaphore_signal(barrier, 1, device_id=(lax.rem(gx + k, ndx), gy), device_id_type=MESH)
    for to in diagonals:
        pl.semaphore_signal(barrier, 1, device_id=to, device_id_type=MESH)

    per_tile = 128 // ny
    tile_count = ndy // per_tile
    tile = gy // per_tile
    row_starts = (
        (0, lax.rem(gx * nx + ndx * nx - 8, ndx * nx), 8),
        (8, gx * nx, nx),
        (8 + nx, lax.rem(gx * nx + nx, ndx * nx), 8),
    )
    loads = [
        pltpu.make_async_copy(binv_any.at[0], binv, load_sem.at[0]),
        pltpu.make_async_copy(right_any.at[0, 0], bases.at[0], load_sem.at[1]),
        pltpu.make_async_copy(left_any.at[0, 0], bases.at[1], load_sem.at[2]),
        pltpu.make_async_copy(right_any.at[1, 0], bases.at[2], load_sem.at[3]),
        pltpu.make_async_copy(left_any.at[1, 0], bases.at[3], load_sem.at[4]),
        pltpu.make_async_copy(b_any, b, load_sem.at[5]),
    ]
    for e in (0, 1):
        for side in (0, 1, 2):
            col = pl.multiple_of(lax.rem(tile + side + tile_count - 1, tile_count) * 128, 128)
            for to, start, count in row_starts:
                loads.append(
                    pltpu.make_async_copy(
                        ranks_any.at[e, 0, pl.ds(pl.multiple_of(start, 8), count), pl.ds(col, 128)],
                        tiles.at[e, side, pl.ds(to, count)],
                        load_sem.at[len(loads)],
                    )
                )
    for load in loads:
        load.start()

    for k in range(3):
        c[k, 0:ny, :] = jnp.zeros((ny, 128), F32)
        c[k, (nx + 1) * ny : (nx + 2) * ny, :] = jnp.zeros((ny, 128), F32)

    for load in loads[:5]:
        load.wait()
    high, low = halves(binv[...].T)
    wb[0:nz, :] = high
    wb[nz : 2 * nz, :] = high
    wb[2 * nz : 3 * nz, :] = low
    factors = bases[...].reshape(4 * 32, nz)
    high, low = halves(factors.T)
    wc[0:nz, 0:128] = high
    wc[0:nz, 128:256] = low
    wc[nz : 2 * nz, 0:128] = high
    wc[nz : 2 * nz, 128:256] = jnp.zeros((nz, 128), BF16)
    swapped = jnp.concatenate([bases[1], bases[0], bases[3], bases[2]], axis=0)
    high, low = halves(swapped)
    wd[0:128, :] = high
    wd[128:256, :] = high
    wd[256:384, :] = low

    def cells(x):
        return pl.ds(pl.multiple_of((x + 1) * ny, ny), ny)

    def flat(i):
        return pl.ds(pl.multiple_of(i * rows, rows), rows)

    def inner(i):
        return pl.ds(pl.multiple_of(i * rows + ny, ny), rows)

    def segments(count):
        return lax.broadcasted_iota(jnp.int32, (count, 128), 1) // 32

    loads[5].wait()

    def put_split(x, value):
        at = pl.ds(pl.multiple_of(x * ny, ny), ny)
        high, low = halves(value)
        split[at, 0:nz] = high
        split[at, nz : 2 * nz] = low

    def put_ends(k, start, first, last):
        here = pl.ds(pl.multiple_of(start, 8), 8)
        raw_send[k, 0, here, :] = jnp.concatenate(first, axis=0)
        raw_send[k, 1, here, :] = jnp.concatenate(last, axis=0)

    def first_split(g, _):
        first, last = [], []
        for j in range(8):
            value = b[g * 8 + j]
            put_split(g * 8 + j, value)
            first.append(value[:1])
            last.append(value[ny - 1 :])
        put_ends(0, g * 8, first, last)
        return 0

    lax.fori_loop(0, nx // 8, first_split, 0)

    def coefs(k, i):
        both = dot(split[flat(i), :], wc[...])
        c[k, inner(i), :] = both[:, :128] + both[:, 128:]

    def pack_y(k, i):
        seg = segments(step)
        base = pl.multiple_of(i * rows + ny, ny)
        first, second = (c[k, pl.ds(base + n, step, stride=ny), :] for n in (0, 1))
        last, before = (c[k, pl.ds(base + ny - n, step, stride=ny), :] for n in (1, 2))
        coef_send[k, pl.ds(pl.multiple_of(2 * ny + i * step, step), step), :] = jnp.where(
            seg == 3, pltpu.roll(second, 32, 1), first
        )
        coef_send[k, pl.ds(pl.multiple_of(2 * ny + nx + i * step, step), step), :] = jnp.where(
            seg == 2, pltpu.roll(before, 96, 1), last
        )

    def pack_x(k, side):
        seg = segments(ny)
        x, behind, where, turn = ((0, 1, 1, 32), (nx - 1, nx - 2, 0, 96))[side]
        own = c[k, cells(x), :]
        coef_send[k, pl.ds(side * ny, ny), :] = jnp.where(seg == where, pltpu.roll(c[k, cells(behind), :], turn, 1), own)
        if k < 2:
            corner_send[k, 2 * (1 - side)] = jnp.broadcast_to(own[ny - 1 :], (8, 128))
            corner_send[k, 2 * (1 - side) + 1] = jnp.broadcast_to(own[:1], (8, 128))

    fields = (b, v0)

    def x_copies(k, side):
        to = ((west, gy), (east, gy))[side]
        mine, theirs = side * ny, (1 - side) * ny
        pairs = [(coef_send.at[k, pl.ds(mine, ny)], coef_recv.at[k, pl.ds(theirs, ny)])]
        if k < 2:
            pairs.append((fields[k].at[(0, nx - 1)[side]], raw_recv.at[k, pl.ds(theirs, ny)]))
        copies = [
            pltpu.make_async_remote_copy(
                src_ref=src, dst_ref=dst, send_sem=xsend_sem.at[k, side, n], recv_sem=xrecv_sem.at[k, side, n],
                device_id=to, device_id_type=MESH,
            )
            for n, (src, dst) in enumerate(pairs)
        ]
        if k < 2:
            for n in (2 * (1 - side), 2 * (1 - side) + 1):
                copies.append(
                    pltpu.make_async_remote_copy(
                        src_ref=corner_send.at[k, n], dst_ref=corner_recv.at[k, n],
                        send_sem=ksend_sem.at[k, n], recv_sem=krecv_sem.at[k, n],
                        device_id=diagonals[n], device_id_type=MESH,
                    )
                )
        return copies

    def y_copies(k, side, i):
        here = pl.ds(pl.multiple_of(i * step, step), step)
        there = pl.ds(pl.multiple_of(2 * ny + side * nx + i * step, step), step)
        pairs = [(coef_send.at[k, there], coef_recv.at[k, there])]
        if k < 2:
            pairs.append((raw_send.at[k, side, here], raw_recv.at[k, there]))
        return [
            pltpu.make_async_remote_copy(
                src_ref=src, dst_ref=dst, send_sem=ysend_sem.at[k, side, n, i], recv_sem=yrecv_sem.at[k, side, n, i],
                device_id=(gx, (south, north)[side]), device_id_type=MESH,
            )
            for n, (src, dst) in enumerate(pairs)
        ]

    def send_chunk(k, turn, i):
        for side in (0, 1):

            @pl.when(turn == side)
            def _():
                pack_x(k, side)
                for copy in x_copies(k, side):
                    copy.start()

        pack_y(k, i)
        for side in (0, 1):
            for copy in y_copies(k, side, i):
                copy.start()

    def all_copies(k):
        return [copy for side in (0, 1) for copy in x_copies(k, side)] + [
            copy for side in (0, 1) for i in range(chunks) for copy in y_copies(k, side, i)
        ]

    def chunk(turn):
        return jnp.where(turn == 0, 0, jnp.where(turn == 1, chunks - 1, turn - 1))

    def diagonal(out, place):
        def body(i, _):
            value = split[flat(i), :]
            out[place(i), :] = dot(jnp.concatenate([value, value[:, :nz]], axis=1), wb[...])
            return 0

        lax.fori_loop(0, chunks, body, 0)

    def couple(k, out, place):
        seg = segments(ny)
        line = lax.broadcasted_iota(jnp.int32, (ny, 128), 0)
        use_after = (seg == 2) & (line < ny - 1)
        use_before = (seg == 3) & (line > 0)

        def body(i, _):
            for j in range(step):
                x = i * step + j
                here = c[k, cells(x), :]
                coef = jnp.where(seg == 0, c[k, cells(x + 1), :], jnp.where(seg == 1, c[k, cells(x - 1), :], 0.0))
                coef = jnp.where(use_after, pltpu.roll(here, ny - 1, 0), coef)
                coef = jnp.where(use_before, pltpu.roll(here, 1, 0), coef)
                coef = coef * mask[pl.ds(pl.multiple_of(x * ny, ny), ny), :]
                high, low = halves(coef)
                dsplit[j * ny : (j + 1) * ny, 0:128] = high
                dsplit[j * ny : (j + 1) * ny, 128:256] = low
            value = dsplit[...]
            out[place(i), :] = out[place(i), :] + dot(jnp.concatenate([value, value[:, :128]], axis=1), wd[...])
            return 0

        lax.fori_loop(0, chunks, body, 0)

    def add_ends(out, at, first, last):
        line = lax.broadcasted_iota(jnp.int32, (8, nz), 0)

        def body(x, _):
            head = pl.ds(pl.multiple_of(at + x * ny, 8), 8)
            tail = pl.ds(pl.multiple_of(at + x * ny + ny - 8, 8), 8)
            more = jnp.broadcast_to(fsplit_out[pl.ds(first + x, 1), :], (8, nz))
            out[head, :] = out[head, :] + jnp.where(line == 0, more, 0.0)
            more = jnp.broadcast_to(fsplit_out[pl.ds(last + x, 1), :], (8, nz))
            out[tail, :] = out[tail, :] + jnp.where(line == 7, more, 0.0)
            return 0

        lax.fori_loop(0, nx, body, 0, unroll=8)

    fsplit_out = uy

    def put_fix(at, value):
        high, low = halves(value)
        fsplit[at : at + value.shape[0], 0:128] = high
        fsplit[at : at + value.shape[0], 128:256] = low

    def fix_own(k):
        put_fix(0, coef_recv[k] * edge_mask[...])

    def fix_halo(k):
        got = lambda at, count: coef_recv[k, at : at + count, :]
        corner = lambda n, count: jnp.broadcast_to(corner_recv[k, n][:1], (count, 128))
        ws, wn, es, en = range(4)
        seg = segments(ny)
        line = lax.broadcasted_iota(jnp.int32, (ny, 128), 0)
        for side, (lo, hi) in enumerate(((ws, wn), (es, en))):
            here = got(side * ny, ny)
            after = jnp.where(line == ny - 1, corner(hi, ny), pltpu.roll(here, ny - 1, 0))
            before = jnp.where(line == 0, corner(lo, ny), pltpu.roll(here, 1, 0))
            if side == 0:
                ahead, behind = c[k, cells(0), :], pltpu.roll(here, 32, 1)
            else:
                ahead, behind = pltpu.roll(here, 96, 1), c[k, cells(nx - 1), :]
            coef = jnp.where(seg == 0, ahead, jnp.where(seg == 1, behind, jnp.where(seg == 2, after, before)))
            put_fix(edge + side * ny, coef * mask[lines + side * ny : lines + (side + 1) * ny, :])
        seg = segments(nx)
        line = lax.broadcasted_iota(jnp.int32, (nx, 128), 0)
        for side, (lo, hi) in enumerate(((wn, en), (ws, es))):
            at = 2 * ny + side * nx
            here = got(at, nx)
            ahead = jnp.where(line == nx - 1, corner(hi, nx), pltpu.roll(here, nx - 1, 0))
            behind = jnp.where(line == 0, corner(lo, nx), pltpu.roll(here, 1, 0))
            if side == 0:
                after = pltpu.roll(here, 96, 1)
                before = c[k, pl.ds(ny + ny - 1, nx, stride=ny), :]
            else:
                after = c[k, pl.ds(ny, nx, stride=ny), :]
                before = pltpu.roll(here, 32, 1)
            coef = jnp.where(seg == 0, ahead, jnp.where(seg == 1, behind, jnp.where(seg == 2, after, before)))
            put_fix(edge + at, coef * mask[lines + at : lines + at + nx, :])

    def finish_field(k, u):
        for copy in all_copies(k):
            copy.wait_recv()
        fix_own(k)
        fix_halo(k)
        high, low = halves(raw_recv[k])
        value = fsplit[...]
        more = dot(jnp.concatenate([value, value[:, :128]], axis=1), wd[...])
        halo = more[edge:] + dot(jnp.concatenate([high, low, high], axis=1), wb[...])
        u[0:ny, :] = halo[:ny]
        u[(nx + 1) * ny : (nx + 2) * ny, :] = halo[ny : 2 * ny]
        uy[0 : 2 * nx, :] = halo[2 * ny :]
        uy[2 * nx : 4 * nx, :] = more[2 * ny : edge]
        u[cells(0), :] = u[cells(0), :] + more[:ny]
        u[cells(nx - 1), :] = u[cells(nx - 1), :] + more[ny : 2 * ny]
        add_ends(u, ny, 3 * nx, 2 * nx)

    zero = jnp.zeros((8, nz), F32)

    def operate(k, u, v, start, sums):
        line = lax.broadcasted_iota(jnp.int32, (ny, nz), 0)

        def body(turn, carry):
            i = chunk(turn)

            def group(g, carry):
                first, last = [], []
                for j in range(8):
                    x = i * step + g * 8 + j
                    here = u[cells(x), :]
                    after = jnp.broadcast_to(uy[pl.ds(x, 1), :], here.shape)
                    before = jnp.broadcast_to(uy[pl.ds(nx + x, 1), :], here.shape)
                    beside = jnp.where(line == ny - 1, after, pltpu.roll(here, ny - 1, 0))
                    beside = beside + jnp.where(line == 0, before, pltpu.roll(here, 1, 0))
                    beside = beside + u[cells(x + 1), :] + u[cells(x - 1), :]
                    beside = beside + pltpu.roll(here, 1, 1) + pltpu.roll(here, nz - 1, 1)
                    value = (6.0 + mass_shift) * here - beside
                    v[x] = value
                    put_split(x, value)
                    first.append(value[:1])
                    last.append(value[ny - 1 :])
                    carry = sums(x, here, value, carry)
                if k < 2:
                    put_ends(k, i * step + g * 8, first, last)
                return carry

            carry = lax.fori_loop(0, step // 8, group, carry)
            coefs(k, i)
            send_chunk(k, turn, i)
            return carry

        return lax.fori_loop(0, chunks, body, start)

    def first_coefs(i, _):
        coefs(0, i)
        return 0

    lax.fori_loop(0, chunks, first_coefs, 0)

    for load in loads[6:]:
        load.wait()
    tall = nx + 16
    lane = lax.broadcasted_iota(jnp.int32, (tall, 128), 1)
    offset = lax.rem(gy, per_tile) * ny - 32
    window = []
    for e in (0, 1):
        below, own, above = (pltpu.roll(tiles[e, side].astype(F32), lax.rem(128 - offset, 128), 1) for side in range(3))
        window.append(jnp.where(lane + offset < 0, below, jnp.where(lane + offset >= 128, above, own)))
    ranks_x, ranks_y = window
    ranks_behind = pltpu.roll(ranks_x, 1, 0)
    wide = jnp.where(
        lane < 32,
        pltpu.roll(ranks_x, 96, 1),
        jnp.where(lane < 64, ranks_behind, jnp.where(lane < 96, pltpu.roll(ranks_y, 32, 1), pltpu.roll(ranks_y, 65, 1))),
    )
    limits[...] = wide
    level = lambda count: lax.rem(lax.broadcasted_iota(jnp.int32, (count, 128), 1), 32).astype(F32)
    for side, y in enumerate((32 + ny, 31)):
        column = lambda table, t: jnp.broadcast_to(table[:, t : t + 1], (tall, 128))
        own_y, back_y = column(ranks_y, y), column(ranks_y, y - 1)
        limit = jnp.where(
            lane < 32,
            column(ranks_x, y),
            jnp.where(lane < 64, column(ranks_behind, y), jnp.where(lane < 96, own_y, back_y)),
        )
        at = lines + 2 * ny + side * nx
        mask[at : at + nx, :] = jnp.where(level(nx) < limit[8 : 8 + nx], 1.0, 0.0)
    own = lax.rem(lax.broadcasted_iota(jnp.int32, (ny, 128), 1), 32) == lax.broadcasted_iota(jnp.int32, (ny, 128), 0)
    spread = (
        lax.broadcasted_iota(jnp.int32, (128, 128), 0) // 32 == lax.broadcasted_iota(jnp.int32, (128, 128), 1) // 32
    ).astype(F32).astype(BF16)

    def place(x, at):
        line_ranks = jnp.broadcast_to(limits[pl.ds(x + 8, 1), :], (ny, 128))
        picks[pl.ds(pl.multiple_of(at * ny, ny), ny), :] = jnp.where(own, line_ranks, 0.0).astype(BF16)

    def place_own(x, _):
        place(x, x)
        return 0

    lax.fori_loop(0, nx, place_own, 0, unroll=4)
    place(-1, nx)
    place(nx, nx + 1)

    def fill_mask(i, _):
        mask[flat(i), :] = jnp.where(level(rows) < dot(picks[flat(i), :], spread), 1.0, 0.0)
        return 0

    lax.fori_loop(0, chunks, fill_mask, 0)
    mask[lines : lines + 2 * ny, :] = jnp.where(level(2 * ny) < dot(picks[lines : lines + 2 * ny, :], spread), 1.0, 0.0)
    edge_mask[0:ny, :] = jnp.where(segments(ny) == 1, mask[0:ny, :], 0.0)
    edge_mask[ny : 2 * ny, :] = jnp.where(segments(ny) == 0, mask[lines - ny : lines, :], 0.0)
    edge_mask[2 * ny : 2 * ny + nx, :] = jnp.where(segments(nx) == 2, mask[pl.ds(ny - 1, nx, stride=ny), :], 0.0)
    edge_mask[2 * ny + nx : edge, :] = jnp.where(segments(nx) == 3, mask[pl.ds(0, nx, stride=ny), :], 0.0)

    diagonal(u0, inner)
    couple(0, u0, inner)
    pl.semaphore_wait(barrier, ndx + ndy + 2)

    def first_send(turn, _):
        send_chunk(0, turn, chunk(turn))
        return 0

    lax.fori_loop(0, chunks, first_send, 0)
    finish_field(0, u0)

    bu0, u0v0 = operate(
        1, u0, v0, (zero, zero),
        lambda x, here, value, carry: (carry[0] + fold(here * b[x]), carry[1] + fold(here * value)),
    )

    diagonal(u1, inner)
    couple(1, u1, inner)
    finish_field(1, u1)

    bu1, v0u1, u1v1 = operate(
        2, u1, v1, (zero, zero, zero),
        lambda x, here, value, carry: (
            carry[0] + fold(here * b[x]), carry[1] + fold(here * v0[x]), carry[2] + fold(here * value),
        ),
    )

    def row_of(value):
        value = value[:, :128] + value[:, 128:]
        return jnp.sum(value, axis=0, keepdims=True)

    partial = jnp.concatenate(
        [row_of(s) for s in (bu0, u0v0, bu1, v0u1, u1v1)] + [jnp.zeros((3, 128), F32)], axis=0
    )
    part[0] = partial
    got_y[gy] = partial
    along_y = [
        pltpu.make_async_remote_copy(
            src_ref=part.at[0], dst_ref=got_y.at[gy], send_sem=rsend_sem.at[0, k], recv_sem=rrecv_sem.at[0, k],
            device_id=(gx, lax.rem(gy + k, ndy)), device_id_type=MESH,
        )
        for k in range(1, ndy)
    ]
    for copy in along_y:
        copy.start()

    diagonal(u2, flat)
    couple(2, u2, flat)
    for copy in along_y:
        copy.wait()
    partial = jnp.sum(got_y[...], axis=0)
    part[1] = partial
    got_x[gx] = partial
    along_x = [
        pltpu.make_async_remote_copy(
            src_ref=part.at[1], dst_ref=got_x.at[gx], send_sem=rsend_sem.at[1, k], recv_sem=rrecv_sem.at[1, k],
            device_id=(lax.rem(gx + k, ndx), gy), device_id_type=MESH,
        )
        for k in range(1, ndx)
    ]
    for copy in along_x:
        copy.start()
    for copy in all_copies(2):
        copy.wait_recv()
    fix_own(2)
    value = fsplit[0:edge, :]
    more = dot(jnp.concatenate([value, value[:, :128]], axis=1), wd[...])
    uy[2 * nx : 4 * nx, :] = more[2 * ny :]
    u2[0:ny, :] = u2[0:ny, :] + more[:ny]
    u2[lines - ny : lines, :] = u2[lines - ny : lines, :] + more[ny : 2 * ny]
    add_ends(u2, 0, 3 * nx, 2 * nx)
    for k in range(3):
        for copy in all_copies(k):
            copy.wait_send()
    for copy in along_x:
        copy.wait()
    total = jnp.sum(jnp.sum(got_x[...], axis=0), axis=1, keepdims=True)
    s = [total[k : k + 1, :] for k in range(5)]

    alpha0 = s[S_BU0] / s[S_U0V0]
    rz1 = s[S_BU0] - alpha0 * (s[S_U0V0] + s[S_BU1]) + alpha0 * (alpha0 * s[S_V0U1])
    grow = 1.0 + rz1 / s[S_BU0]
    curve = grow * (grow * s[S_U0V0] - 2.0 * (alpha0 * s[S_V0U1])) + alpha0 * (alpha0 * s[S_U1V1])
    alpha1 = rz1 / curve
    on0 = alpha0 + alpha1 * grow
    on1 = -(alpha1 * alpha0)
    scale[0] = jnp.broadcast_to(on0, (8, 128))
    scale[1] = jnp.broadcast_to(on1, (8, 128))


def combine(b, u0, u1, u2, v0, v1, scale, x_any, gap_any, z_any, x_out, gap_out, z_out, sem):
    nx, ny, nz = x_out.shape
    step = 8
    on0, on1 = (jnp.concatenate([jnp.concatenate([scale[k]] * 2, axis=1)] * (ny // 8), axis=0) for k in (0, 1))

    def copies(i):
        here = pl.ds(pl.multiple_of(i * step, step), step)
        return [
            pltpu.make_async_copy(out.at[here], out_any.at[here], sem.at[n, i])
            for n, (out, out_any) in enumerate(((x_out, x_any), (z_out, z_any), (gap_out, gap_any)))
        ]

    def body(i, _):
        for j in range(step):
            x = i * step + j
            at = pl.ds(pl.multiple_of((x + 1) * ny, ny), ny)
            f0, f1 = u0[at, :], u1[at, :]
            x_out[x] = on0 * f0 + on1 * f1
            z_out[x] = f0 - on0 * f1 - on1 * u2[pl.ds(pl.multiple_of(x * ny, ny), ny), :]
            gap_out[x] = b[x] - on0 * v0[x] - on1 * v1[x]
        for copy in copies(i):
            copy.start()
        return 0

    lax.fori_loop(0, nx // step, body, 0)

    def finish(i, _):
        for copy in copies(i):
            copy.wait()
        return 0

    lax.fori_loop(0, nx // step, finish, 0)


def per_device(devs, right_side, block_inverse, basis_left, basis_right, ranks):
    nx, ny, nz = right_side.shape
    ndx, ndy = devs
    lines = nx * ny
    padded = lines + 2 * ny
    edge = 2 * (nx + ny)
    block = jax.ShapeDtypeStruct(right_side.shape, F32)
    framed = jax.ShapeDtypeStruct((padded, nz), F32)
    arrays = (right_side, block_inverse, basis_left, basis_right, ranks)
    fields = pl.pallas_call(
        functools.partial(kernel, devs),
        out_shape=(
            block, framed, framed, jax.ShapeDtypeStruct((lines, nz), F32), block, block,
            jax.ShapeDtypeStruct((2, 8, 128), F32),
        ),
        in_specs=[pl.BlockSpec(memory_space=pltpu.HBM)] * 5,
        out_specs=[pl.BlockSpec(memory_space=pltpu.VMEM)] * 7,
        scratch_shapes=[
            pltpu.VMEM((nz, nz), F32),
            pltpu.VMEM((4, 32, nz), F32),
            pltpu.VMEM((2, 3, nx + 16, 128), jnp.int32),
            pltpu.VMEM((nx + 16, 128), F32),
            pltpu.VMEM((lines + 2 * ny, 128), BF16),
            pltpu.VMEM((3 * nz, nz), BF16),
            pltpu.VMEM((2 * nz, 256), BF16),
            pltpu.VMEM((384, nz), BF16),
            pltpu.VMEM((lines + edge, 128), F32),
            pltpu.VMEM((edge, 128), F32),
            pltpu.VMEM((lines, 2 * nz), BF16),
            pltpu.VMEM((16 * ny, 256), BF16),
            pltpu.VMEM((2 * edge, 256), BF16),
            pltpu.VMEM((3, padded, 128), F32),
            pltpu.VMEM((3, edge, 128), F32),
            pltpu.VMEM((3, edge, 128), F32),
            pltpu.VMEM((2, 2, nx, nz), F32),
            pltpu.VMEM((2, edge, nz), F32),
            pltpu.VMEM((2, 4, 8, 128), F32),
            pltpu.VMEM((2, 4, 8, 128), F32),
            pltpu.VMEM((4 * nx, nz), F32),
            pltpu.VMEM((2, 8, 128), F32),
            pltpu.VMEM((ndy, 8, 128), F32),
            pltpu.VMEM((ndx, 8, 128), F32),
            pltpu.SemaphoreType.DMA((24,)),
            pltpu.SemaphoreType.DMA((3, 2, 2)),
            pltpu.SemaphoreType.DMA((3, 2, 2)),
            pltpu.SemaphoreType.DMA((3, 2, 2, nx // 16)),
            pltpu.SemaphoreType.DMA((3, 2, 2, nx // 16)),
            pltpu.SemaphoreType.DMA((2, 4)),
            pltpu.SemaphoreType.DMA((2, 4)),
            pltpu.SemaphoreType.DMA((2, ndy)),
            pltpu.SemaphoreType.DMA((2, ndy)),
        ],
        compiler_params=pltpu.CompilerParams(
            collective_id=0, has_side_effects=True, vmem_limit_bytes=32 * 1024 * 1024
        ),
    )(*(pltpu.with_memory_space_constraint(array, pltpu.HBM) for array in arrays))
    return pl.pallas_call(
        combine,
        out_shape=(block, block, block),
        in_specs=[pl.BlockSpec(memory_space=pltpu.VMEM)] * 7,
        out_specs=[pl.BlockSpec(memory_space=pltpu.HBM)] * 3,
        scratch_shapes=[pltpu.VMEM((nx, ny, nz), F32)] * 3 + [pltpu.SemaphoreType.DMA((3, nx // 8))],
        compiler_params=pltpu.CompilerParams(vmem_limit_bytes=32 * 1024 * 1024),
    )(*fields)


def solution(mesh):
    devs = (mesh.shape["gx"], mesh.shape["gy"])
    return jax.shard_map(
        functools.partial(per_device, devs),
        mesh=mesh,
        in_specs=(P("gx", "gy", None), P(), P(), P(), P()),
        out_specs=(P("gx", "gy", None),) * 3,
        check_vma=False,
    )
```

time: 45.9 us -> 46.4 us (1.011)
  Pallas kernels: 45 us -> 45.5 us
    pallas_call x1, Pallas kernels: 42.1 us -> 42.7 us  [per_device(): pl.pallas_call(functools.partial(kernel, devs), out_shape=(block, framed,...]
where the time goes in v2:
time: 46.4 us; the launch traced here: 46.2 us
  Pallas kernels  45.5 us (98%)
  between operations  0.64 us (1%)
    pallas_call x1, Pallas kernels, per_device(): pl.pallas_call(functools.partial(kernel, devs), out_shape=(block, framed,...  42.7 us
    pallas_call x1, Pallas kernels, per_device(): pl.pallas_call(combine, out_shape=(block, block, block), in_specs=[pl.Blo...  2.89 us

profile of v2, /device:TPU:0, one launch (start us, length us, event | category | flops | bytes accessed | tf_op | source)
XLA Modules:
  0.0 46.2 jit_solution(4028972509650772789)
XLA Ops:
  0.6 42.7 %shard_map.76 = (f32[64,32,256]{2,1,0:T(8,128)S(1)}, f32[2112,256]{1,0:T(8,128)S(1)}, f32[2112,256]{1,0:T(8,128)S(1)}, f32[2048,256]{1,0:T(8,128)S(1)}, f32[64,3...) custom-call(f32[64,32,256]{2,1,0:T(8,128)} %b_any.1, f32[1,256,256]{2,1,0:T(8,128)} %binv_any.1, ...), custom_call_target="tpu_custom_call" | custom-call | tf_op jit(solution)/shard_map/pallas_call | solution.py:572
  43.3 2.9 %shard_map.77 = (f32[64,32,256]{2,1,0:T(8,128)}, f32[64,32,256]{2,1,0:T(8,128)}, f32[64,32,256]{2,1,0:T(8,128)}) custom-call(f32[64,32,256]{2,1,0:T(8,128)S(1)} %get-tuple-element.10.b, f32[2112,256]{1,0:T(8,128)S(1)} %get-tuple-element.11.u0, f32[2112,256]{1,0:T(8,128)S(1)} %get-tuple-element.12.u1, f32[2048,256]{1,0:T(8,128)S(1)} %get-tuple-element.13.u2, ...), custom_call_target="tpu_custom_call" | custom-call | tf_op jit(solution)/shard_map/pallas_call | solution.py:619

commit v3 on v2

--- a/solution.py
+++ b/solution.py
@@ -88,39 +88,26 @@
     for load in loads:
         load.start()
 
-    for k in range(3):
-        c[k, 0:ny, :] = jnp.zeros((ny, 128), F32)
-        c[k, (nx + 1) * ny : (nx + 2) * ny, :] = jnp.zeros((ny, 128), F32)
-
-    for load in loads[:5]:
+    def cells(x):
+        return pl.ds(pl.multiple_of((x + 1) * ny, ny), ny)
+
+    def flat(i):
+        return pl.ds(pl.multiple_of(i * rows, rows), rows)
+
+    def inner(i):
+        return pl.ds(pl.multiple_of(i * rows + ny, ny), rows)
+
+    def segments(count):
+        return lax.broadcasted_iota(jnp.int32, (count, 128), 1) // 32
+
+    for load in loads[1:5]:
         load.wait()
-    high, low = halves(binv[...].T)
-    wb[0:nz, :] = high
-    wb[nz : 2 * nz, :] = high
-    wb[2 * nz : 3 * nz, :] = low
     factors = bases[...].reshape(4 * 32, nz)
     high, low = halves(factors.T)
     wc[0:nz, 0:128] = high
     wc[0:nz, 128:256] = low
     wc[nz : 2 * nz, 0:128] = high
     wc[nz : 2 * nz, 128:256] = jnp.zeros((nz, 128), BF16)
-    swapped = jnp.concatenate([bases[1], bases[0], bases[3], bases[2]], axis=0)
-    high, low = halves(swapped)
-    wd[0:128, :] = high
-    wd[128:256, :] = high
-    wd[256:384, :] = low
-
-    def cells(x):
-        return pl.ds(pl.multiple_of((x + 1) * ny, ny), ny)
-
-    def flat(i):
-        return pl.ds(pl.multiple_of(i * rows, rows), rows)
-
-    def inner(i):
-        return pl.ds(pl.multiple_of(i * rows + ny, ny), rows)
-
-    def segments(count):
-        return lax.broadcasted_iota(jnp.int32, (count, 128), 1) // 32
 
     loads[5].wait()
 
@@ -199,8 +186,9 @@
         return copies
 
     def y_copies(k, side, i):
-        here = pl.ds(pl.multiple_of(i * step, step), step)
-        there = pl.ds(pl.multiple_of(2 * ny + side * nx + i * step, step), step)
+        count = nx if k == 0 else step
+        here = pl.ds(pl.multiple_of(i * count, step), count)
+        there = pl.ds(pl.multiple_of(2 * ny + side * nx + i * count, step), count)
         pairs = [(coef_send.at[k, there], coef_recv.at[k, there])]
         if k < 2:
             pairs.append((raw_send.at[k, side, here], raw_recv.at[k, there]))
@@ -228,7 +216,7 @@
 
     def all_copies(k):
         return [copy for side in (0, 1) for copy in x_copies(k, side)] + [
-            copy for side in (0, 1) for i in range(chunks) for copy in y_copies(k, side, i)
+            copy for side in (0, 1) for i in range(1 if k == 0 else chunks) for copy in y_copies(k, side, i)
         ]
 
     def chunk(turn):
@@ -376,9 +364,31 @@
 
     def first_coefs(i, _):
         coefs(0, i)
+        pack_y(0, i)
         return 0
 
     lax.fori_loop(0, chunks, first_coefs, 0)
+    for side in (0, 1):
+        pack_x(0, side)
+
+    pl.semaphore_wait(barrier, ndx + ndy + 2)
+    for copy in all_copies(0):
+        copy.start()
+
+    loads[0].wait()
+    high, low = halves(binv[...].T)
+    wb[0:nz, :] = high
+    wb[nz : 2 * nz, :] = high
+    wb[2 * nz : 3 * nz, :] = low
+    swapped = jnp.concatenate([bases[1], bases[0], bases[3], bases[2]], axis=0)
+    high, low = halves(swapped)
+    wd[0:128, :] = high
+    wd[128:256, :] = high
+    wd[256:384, :] = low
+
+    for k in range(3):
+        c[k, 0:ny, :] = jnp.zeros((ny, 128), F32)
+        c[k, (nx + 1) * ny : (nx + 2) * ny, :] = jnp.zeros((ny, 128), F32)
 
     for load in loads[6:]:
         load.wait()
@@ -438,13 +448,6 @@
 
     diagonal(u0, inner)
     couple(0, u0, inner)
-    pl.semaphore_wait(barrier, ndx + ndy + 2)
-
-    def first_send(turn, _):
-        send_chunk(0, turn, chunk(turn))
-        return 0
-
-    lax.fori_loop(0, chunks, first_send, 0)
     finish_field(0, u0)
 
     bu0, u0v0 = operate(

time: 46.4 us -> 42.7 us (0.920)
  Pallas kernels: 45.5 us -> 41.8 us
    pallas_call x1, Pallas kernels: 42.7 us -> 38.9 us  [per_device(): pl.pallas_call(functools.partial(kernel, devs), out_shape=(block, framed,...]
where the time goes in v3:
time: 42.7 us; the launch traced here: 42.5 us
  Pallas kernels  41.8 us (98%)
  between operations  0.64 us (1%)
    pallas_call x1, Pallas kernels, per_device(): pl.pallas_call(functools.partial(kernel, devs), out_shape=(block, framed,...  38.9 us
    pallas_call x1, Pallas kernels, per_device(): pl.pallas_call(combine, out_shape=(block, block, block), in_specs=[pl.Blo...  2.89 us

profile of v3, /device:TPU:0, one launch (start us, length us, event | category | flops | bytes accessed | tf_op | source)
XLA Modules:
  0.0 42.5 jit_solution(5550623767623789253)
XLA Ops:
  0.6 38.9 %shard_map.76 = (f32[64,32,256]{2,1,0:T(8,128)S(1)}, f32[2112,256]{1,0:T(8,128)S(1)}, f32[2112,256]{1,0:T(8,128)S(1)}, f32[2048,256]{1,0:T(8,128)S(1)}, f32[64,3...) custom-call(f32[64,32,256]{2,1,0:T(8,128)} %b_any.1, f32[1,256,256]{2,1,0:T(8,128)} %binv_any.1, ...), custom_call_target="tpu_custom_call" | custom-call | tf_op jit(solution)/shard_map/pallas_call | solution.py:575
  39.6 2.9 %shard_map.77 = (f32[64,32,256]{2,1,0:T(8,128)}, f32[64,32,256]{2,1,0:T(8,128)}, f32[64,32,256]{2,1,0:T(8,128)}) custom-call(f32[64,32,256]{2,1,0:T(8,128)S(1)} %get-tuple-element.10.b, f32[2112,256]{1,0:T(8,128)S(1)} %get-tuple-element.11.u0, f32[2112,256]{1,0:T(8,128)S(1)} %get-tuple-element.12.u1, f32[2048,256]{1,0:T(8,128)S(1)} %get-tuple-element.13.u2, ...), custom_call_target="tpu_custom_call" | custom-call | tf_op jit(solution)/shard_map/pallas_call | solution.py:622

commit v4 on v3

--- a/solution.py
+++ b/solution.py
@@ -49,14 +49,6 @@
     east, west = lax.rem(gx + 1, ndx), lax.rem(gx + ndx - 1, ndx)
     north, south = lax.rem(gy + 1, ndy), lax.rem(gy + ndy - 1, ndy)
     diagonals = ((east, north), (east, south), (west, north), (west, south))
-
-    barrier = pltpu.get_barrier_semaphore()
-    for k in range(1, ndy):
-        pl.semaphore_signal(barrier, 1, device_id=(gx, lax.rem(gy + k, ndy)), device_id_type=MESH)
-    for k in range(1, ndx):
-        pl.semaphore_signal(barrier, 1, device_id=(lax.rem(gx + k, ndx), gy), device_id_type=MESH)
-    for to in diagonals:
-        pl.semaphore_signal(barrier, 1, device_id=to, device_id_type=MESH)
 
     per_tile = 128 // ny
     tile_count = ndy // per_tile
@@ -85,7 +77,18 @@
                         load_sem.at[len(loads)],
                     )
                 )
-    for load in loads:
+    for load in loads[1:6]:
+        load.start()
+
+    barrier = pltpu.get_barrier_semaphore()
+    for k in range(1, ndy):
+        pl.semaphore_signal(barrier, 1, device_id=(gx, lax.rem(gy + k, ndy)), device_id_type=MESH)
+    for k in range(1, ndx):
+        pl.semaphore_signal(barrier, 1, device_id=(lax.rem(gx + k, ndx), gy), device_id_type=MESH)
+    for to in diagonals:
+        pl.semaphore_signal(barrier, 1, device_id=to, device_id_type=MESH)
+
+    for load in loads[:1] + loads[6:]:
         load.start()
 
     def cells(x):
@@ -230,13 +233,13 @@
 
         lax.fori_loop(0, chunks, body, 0)
 
-    def couple(k, out, place):
+    def couple(k, out, place, start=0, sums=None):
         seg = segments(ny)
         line = lax.broadcasted_iota(jnp.int32, (ny, 128), 0)
         use_after = (seg == 2) & (line < ny - 1)
         use_before = (seg == 3) & (line > 0)
 
-        def body(i, _):
+        def body(i, carry):
             for j in range(step):
                 x = i * step + j
                 here = c[k, cells(x), :]
@@ -248,26 +251,23 @@
                 dsplit[j * ny : (j + 1) * ny, 0:128] = high
                 dsplit[j * ny : (j + 1) * ny, 128:256] = low
             value = dsplit[...]
-            out[place(i), :] = out[place(i), :] + dot(jnp.concatenate([value, value[:, :128]], axis=1), wd[...])
-            return 0
-
-        lax.fori_loop(0, chunks, body, 0)
+            total = out[place(i), :] + dot(jnp.concatenate([value, value[:, :128]], axis=1), wd[...])
+            out[place(i), :] = total
+            if sums is not None:
+                for j in range(step):
+                    carry = sums(i * step + j, total[j * ny : (j + 1) * ny, :], carry)
+            return carry
+
+        return lax.fori_loop(0, chunks, body, start)
 
     def add_ends(out, at, first, last):
         line = lax.broadcasted_iota(jnp.int32, (8, nz), 0)
-
-        def body(x, _):
-            head = pl.ds(pl.multiple_of(at + x * ny, 8), 8)
-            tail = pl.ds(pl.multiple_of(at + x * ny + ny - 8, 8), 8)
-            more = jnp.broadcast_to(fsplit_out[pl.ds(first + x, 1), :], (8, nz))
-            out[head, :] = out[head, :] + jnp.where(line == 0, more, 0.0)
-            more = jnp.broadcast_to(fsplit_out[pl.ds(last + x, 1), :], (8, nz))
-            out[tail, :] = out[tail, :] + jnp.where(line == 7, more, 0.0)
-            return 0
-
-        lax.fori_loop(0, nx, body, 0, unroll=8)
-
-    fsplit_out = uy
+        for x in range(nx):
+            head, tail = at + x * ny, at + x * ny + ny - 8
+            more = jnp.broadcast_to(uy[first + x : first + x + 1, :], (8, nz))
+            out[head : head + 8, :] = out[head : head + 8, :] + jnp.where(line == 0, more, 0.0)
+            more = jnp.broadcast_to(uy[last + x : last + x + 1, :], (8, nz))
+            out[tail : tail + 8, :] = out[tail : tail + 8, :] + jnp.where(line == 7, more, 0.0)
 
     def put_fix(at, value):
         high, low = halves(value)
@@ -325,24 +325,25 @@
         u[cells(0), :] = u[cells(0), :] + more[:ny]
         u[cells(nx - 1), :] = u[cells(nx - 1), :] + more[ny : 2 * ny]
         add_ends(u, ny, 3 * nx, 2 * nx)
+        return more[:edge]
 
     zero = jnp.zeros((8, nz), F32)
 
-    def operate(k, u, v, start, sums):
-        line = lax.broadcasted_iota(jnp.int32, (ny, nz), 0)
+    def operate(k, u, v, start, sums, after_chunk):
+        top = lax.broadcasted_iota(jnp.int32, (8, nz), 0)
 
         def body(turn, carry):
             i = chunk(turn)
 
-            def group(g, carry):
+            for g in range(step // 8):
                 first, last = [], []
                 for j in range(8):
                     x = i * step + g * 8 + j
                     here = u[cells(x), :]
-                    after = jnp.broadcast_to(uy[pl.ds(x, 1), :], here.shape)
-                    before = jnp.broadcast_to(uy[pl.ds(nx + x, 1), :], here.shape)
-                    beside = jnp.where(line == ny - 1, after, pltpu.roll(here, ny - 1, 0))
-                    beside = beside + jnp.where(line == 0, before, pltpu.roll(here, 1, 0))
+                    up, down = pltpu.roll(here, ny - 1, 0), pltpu.roll(here, 1, 0)
+                    after = jnp.where(top == 7, jnp.broadcast_to(uy[pl.ds(x, 1), :], (8, nz)), up[ny - 8 :])
+                    before = jnp.where(top == 0, jnp.broadcast_to(uy[pl.ds(nx + x, 1), :], (8, nz)), down[:8])
+                    beside = jnp.concatenate([up[: ny - 8], after], axis=0) + jnp.concatenate([before, down[8:]], axis=0)
                     beside = beside + u[cells(x + 1), :] + u[cells(x - 1), :]
                     beside = beside + pltpu.roll(here, 1, 1) + pltpu.roll(here, nz - 1, 1)
                     value = (6.0 + mass_shift) * here - beside
@@ -353,14 +354,17 @@
                     carry = sums(x, here, value, carry)
                 if k < 2:
                     put_ends(k, i * step + g * 8, first, last)
-                return carry
-
-            carry = lax.fori_loop(0, step // 8, group, carry)
+            after_chunk(turn, i)
+            return carry
+
+        return lax.fori_loop(0, chunks, body, start)
+
+    def coefs_and_send(k):
+        def go(turn, i):
             coefs(k, i)
             send_chunk(k, turn, i)
-            return carry
-
-        return lax.fori_loop(0, chunks, body, start)
+
+        return go
 
     def first_coefs(i, _):
         coefs(0, i)
@@ -450,20 +454,31 @@
     couple(0, u0, inner)
     finish_field(0, u0)
 
-    bu0, u0v0 = operate(
-        1, u0, v0, (zero, zero),
-        lambda x, here, value, carry: (carry[0] + fold(here * b[x]), carry[1] + fold(here * value)),
+    operate(1, u0, v0, 0, lambda x, here, value, carry: carry, coefs_and_send(1))
+
+    diagonal(u1, inner)
+
+    def early(x, total, carry):
+        have = u0[cells(x), :]
+        return (
+            carry[0] + fold(have * b[x]), carry[1] + fold(have * v0[x]),
+            carry[2] + fold(total * b[x]), carry[3] + fold(total * v0[x]),
+        )
+
+    bu0, u0v0, bu1, v0u1 = couple(1, u1, inner, (zero, zero, zero, zero), early)
+    more = finish_field(1, u1)
+    pieces = (
+        (more[:ny], lambda k: fields[k][0]),
+        (more[ny : 2 * ny], lambda k: fields[k][nx - 1]),
+        (more[2 * ny : 2 * ny + nx], lambda k: raw_send[k, 1]),
+        (more[2 * ny + nx :], lambda k: raw_send[k, 0]),
     )
-
-    diagonal(u1, inner)
-    couple(1, u1, inner)
-    finish_field(1, u1)
-
-    bu1, v0u1, u1v1 = operate(
-        2, u1, v1, (zero, zero, zero),
-        lambda x, here, value, carry: (
-            carry[0] + fold(here * b[x]), carry[1] + fold(here * v0[x]), carry[2] + fold(here * value),
-        ),
+    for piece, line_of in pieces:
+        bu1 = bu1 + fold(piece * line_of(0))
+        v0u1 = v0u1 + fold(piece * line_of(1))
+
+    u1v1 = operate(
+        2, u1, v1, zero, lambda x, here, value, carry: carry + fold(here * value), lambda turn, i: None
     )
 
     def row_of(value):
@@ -485,6 +500,11 @@
     for copy in along_y:
         copy.start()
 
+    def last_send(turn, _):
+        coefs_and_send(2)(turn, chunk(turn))
+        return 0
+
+    lax.fori_loop(0, chunks, last_send, 0)
     diagonal(u2, flat)
     couple(2, u2, flat)
     for copy in along_y:

time: 42.7 us -> 38.9 us (0.911)
  Pallas kernels: 41.8 us -> 38 us
    pallas_call x1, Pallas kernels: 38.9 us -> 35.2 us  [per_device(): pl.pallas_call(functools.partial(kernel, devs), out_shape=(block, framed,...]
where the time goes in v4:
time: 38.9 us; the launch traced here: 38.7 us
  Pallas kernels  38 us (98%)
  between operations  0.64 us (2%)
    pallas_call x1, Pallas kernels, per_device(): pl.pallas_call(functools.partial(kernel, devs), out_shape=(block, framed,...  35.2 us
    pallas_call x1, Pallas kernels, per_device(): pl.pallas_call(combine, out_shape=(block, block, block), in_specs=[pl.Blo...  2.89 us

profile of v4, /device:TPU:0, one launch (start us, length us, event | category | flops | bytes accessed | tf_op | source)
XLA Modules:
  0.0 38.7 jit_solution(15836425251134917884)
XLA Ops:
  0.6 35.2 %shard_map.76 = (f32[64,32,256]{2,1,0:T(8,128)S(1)}, f32[2112,256]{1,0:T(8,128)S(1)}, f32[2112,256]{1,0:T(8,128)S(1)}, f32[2048,256]{1,0:T(8,128)S(1)}, f32[64,3...) custom-call(f32[64,32,256]{2,1,0:T(8,128)} %b_any.1, f32[1,256,256]{2,1,0:T(8,128)} %binv_any.1, ...), custom_call_target="tpu_custom_call" | custom-call | tf_op jit(solution)/shard_map/pallas_call | solution.py:595
  35.8 2.9 %shard_map.77 = (f32[64,32,256]{2,1,0:T(8,128)}, f32[64,32,256]{2,1,0:T(8,128)}, f32[64,32,256]{2,1,0:T(8,128)}) custom-call(f32[64,32,256]{2,1,0:T(8,128)S(1)} %get-tuple-element.10.b, f32[2112,256]{1,0:T(8,128)S(1)} %get-tuple-element.11.u0, f32[2112,256]{1,0:T(8,128)S(1)} %get-tuple-element.12.u1, f32[2048,256]{1,0:T(8,128)S(1)} %get-tuple-element.13.u2, ...), custom_call_target="tpu_custom_call" | custom-call | tf_op jit(solution)/shard_map/pallas_call | solution.py:642

commit v5 on v4

--- a/solution.py
+++ b/solution.py
@@ -376,7 +376,8 @@
         pack_x(0, side)
 
     pl.semaphore_wait(barrier, ndx + ndy + 2)
-    for copy in all_copies(0):
+    ends_x = [x_copies(0, side) for side in (0, 1)]
+    for copy in ends_x[0][2:] + ends_x[1][2:] + y_copies(0, 0, 0) + y_copies(0, 1, 0) + ends_x[0][:2] + ends_x[1][:2]:
         copy.start()
 
     loads[0].wait()

time: 38.9 us -> 38.3 us (0.985)
  Pallas kernels: 38 us -> 37.5 us
    pallas_call x1, Pallas kernels: 35.2 us -> 34.6 us  [per_device(): pl.pallas_call(functools.partial(kernel, devs), out_shape=(block, framed,...]
where the time goes in v5:
time: 38.3 us; the launch traced here: 38.1 us
  Pallas kernels  37.5 us (98%)
  between operations  0.64 us (2%)
    pallas_call x1, Pallas kernels, per_device(): pl.pallas_call(functools.partial(kernel, devs), out_shape=(block, framed,...  34.6 us
    pallas_call x1, Pallas kernels, per_device(): pl.pallas_call(combine, out_shape=(block, block, block), in_specs=[pl.Blo...  2.89 us

profile of v5, /device:TPU:0, one launch (start us, length us, event | category | flops | bytes accessed | tf_op | source)
XLA Modules:
  0.0 38.1 jit_solution(7930862730303968615)
XLA Ops:
  0.6 34.6 %shard_map.76 = (f32[64,32,256]{2,1,0:T(8,128)S(1)}, f32[2112,256]{1,0:T(8,128)S(1)}, f32[2112,256]{1,0:T(8,128)S(1)}, f32[2048,256]{1,0:T(8,128)S(1)}, f32[64,3...) custom-call(f32[64,32,256]{2,1,0:T(8,128)} %b_any.1, f32[1,256,256]{2,1,0:T(8,128)} %binv_any.1, ...), custom_call_target="tpu_custom_call" | custom-call | tf_op jit(solution)/shard_map/pallas_call | solution.py:596
  35.2 2.9 %shard_map.77 = (f32[64,32,256]{2,1,0:T(8,128)}, f32[64,32,256]{2,1,0:T(8,128)}, f32[64,32,256]{2,1,0:T(8,128)}) custom-call(f32[64,32,256]{2,1,0:T(8,128)S(1)} %get-tuple-element.10.b, f32[2112,256]{1,0:T(8,128)S(1)} %get-tuple-element.11.u0, f32[2112,256]{1,0:T(8,128)S(1)} %get-tuple-element.12.u1, f32[2048,256]{1,0:T(8,128)S(1)} %get-tuple-element.13.u2, ...), custom_call_target="tpu_custom_call" | custom-call | tf_op jit(solution)/shard_map/pallas_call | solution.py:643

commit v6 on v5

--- a/solution.py
+++ b/solution.py
@@ -209,7 +209,8 @@
             @pl.when(turn == side)
             def _():
                 pack_x(k, side)
-                for copy in x_copies(k, side):
+                copies = x_copies(k, side)
+                for copy in copies[2:] + copies[:2]:
                     copy.start()
 
         pack_y(k, i)
@@ -552,7 +553,7 @@
 
 def combine(b, u0, u1, u2, v0, v1, scale, x_any, gap_any, z_any, x_out, gap_out, z_out, sem):
     nx, ny, nz = x_out.shape
-    step = 8
+    step = 4
     on0, on1 = (jnp.concatenate([jnp.concatenate([scale[k]] * 2, axis=1)] * (ny // 8), axis=0) for k in (0, 1))
 
     def copies(i):
@@ -645,7 +646,7 @@
         out_shape=(block, block, block),
         in_specs=[pl.BlockSpec(memory_space=pltpu.VMEM)] * 7,
         out_specs=[pl.BlockSpec(memory_space=pltpu.HBM)] * 3,
-        scratch_shapes=[pltpu.VMEM((nx, ny, nz), F32)] * 3 + [pltpu.SemaphoreType.DMA((3, nx // 8))],
+        scratch_shapes=[pltpu.VMEM((nx, ny, nz), F32)] * 3 + [pltpu.SemaphoreType.DMA((3, nx // 4))],
         compiler_params=pltpu.CompilerParams(vmem_limit_bytes=32 * 1024 * 1024),
     )(*fields)
 

time: 38.3 us -> 38.4 us (level)
  no operation moved by 1% of the time
where the time goes in v6:
time: 38.4 us; the launch traced here: 38.3 us
  Pallas kernels  37.6 us (98%)
  between operations  0.64 us (2%)
    pallas_call x1, Pallas kernels, per_device(): pl.pallas_call(functools.partial(kernel, devs), out_shape=(block, framed,...  34.6 us
    pallas_call x1, Pallas kernels, per_device(): pl.pallas_call(combine, out_shape=(block, block, block), in_specs=[pl.Blo...  3.06 us

profile of v6, /device:TPU:0, one launch (start us, length us, event | category | flops | bytes accessed | tf_op | source)
XLA Modules:
  0.0 38.3 jit_solution(12758352406225591902)
XLA Ops:
  0.6 34.6 %shard_map.76 = (f32[64,32,256]{2,1,0:T(8,128)S(1)}, f32[2112,256]{1,0:T(8,128)S(1)}, f32[2112,256]{1,0:T(8,128)S(1)}, f32[2048,256]{1,0:T(8,128)S(1)}, f32[64,3...) custom-call(f32[64,32,256]{2,1,0:T(8,128)} %b_any.1, f32[1,256,256]{2,1,0:T(8,128)} %binv_any.1, ...), custom_call_target="tpu_custom_call" | custom-call | tf_op jit(solution)/shard_map/pallas_call | solution.py:597
  35.2 3.1 %shard_map.77 = (f32[64,32,256]{2,1,0:T(8,128)}, f32[64,32,256]{2,1,0:T(8,128)}, f32[64,32,256]{2,1,0:T(8,128)}) custom-call(f32[64,32,256]{2,1,0:T(8,128)S(1)} %get-tuple-element.10.b, f32[2112,256]{1,0:T(8,128)S(1)} %get-tuple-element.11.u0, f32[2112,256]{1,0:T(8,128)S(1)} %get-tuple-element.12.u1, f32[2048,256]{1,0:T(8,128)S(1)} %get-tuple-element.13.u2, ...), custom_call_target="tpu_custom_call" | custom-call | tf_op jit(solution)/shard_map/pallas_call | solution.py:644
